TPU v7x, 128 devices: a whole 4x4x4 slice. The times are simulated.
128 devices in a mesh: rowa: 2 (over x_hi), rowb: 16 (over z, y), col: 4 (over x_lo, core).
Axes of the slice: x: 4 (x_hi: 2, x_lo: 2; x = x_hi * 2 + x_lo), y: 4, z: 4, core: 2. Of those that a mesh axis runs over, the one named last changes fastest.
Arguments:
- table: float32 [262144, 512], P(('rowa', 'rowb'), 'col'), may hold values from -12 to 12
- start: float32 [16, 512], P(None, 'col'), may hold values from -6 to 6
Outputs:
- right_vectors: float32 [16, 512], P(None, 'col')
- left_images: float32 [16, 262144], P(None, ('rowa', 'rowb'))
- strengths: float32 [16], replicated
All inputs are finite; a program needn't handle non-finite values.
Results may differ from a plain program's by a relative error of at most 0.00014.
Values sent between devices are 32-bit elements.
A program may use at most 64 MiB of HBM per device.

v0:
```python
import jax
import jax.numpy as jnp
from jax import lax
from jax.sharding import PartitionSpec as P

STEPS = 8


high = lax.Precision.HIGHEST


def joined_along(pieces, dim):
    lengths = list(pieces.shape[1:])
    lengths[dim] *= pieces.shape[0]
    return jnp.moveaxis(pieces, 0, dim).reshape(lengths)


def from_everyone(x, axis):
    length = lax.axis_size(axis)
    return lax.all_to_all(jnp.broadcast_to(x[None], (length, *x.shape)), axis, 0, 0, tiled=True)


def gather_directly(x, axis, dim):
    return joined_along(from_everyone(x, axis), dim)


def apply_rows(vectors, table):
    return lax.dot_general(
        vectors, table, (((1,), (1,)), ((), ())), precision=high, preferred_element_type=jnp.float32
    )


def outer_gram(products):
    return lax.dot_general(
        products,
        products,
        (((1,), (1,)), ((), ())),
        precision=high,
        preferred_element_type=jnp.float32,
    )


def normalize(gram, products):
    lower = jnp.linalg.cholesky(gram)
    return (jax.scipy.linalg.solve_triangular(lower, products, lower=True), lower)


def own_columns(vectors, start):
    width = start.shape[1]
    offset = lax.axis_index("col") * width
    return lax.dynamic_slice_in_dim(vectors, offset, width, 1)


def on_device(table, start):
    regrouped = lax.all_to_all(table, "col", split_axis=0, concat_axis=1, tiled=True)
    rows_total = table.shape[0] * lax.axis_size("rowa") * lax.axis_size("rowb")
    vectors = gather_directly(start, "col", 1)
    partial_cover = lax.dot_general(
        regrouped,
        regrouped,
        (((0,), (0,)), ((), ())),
        precision=high,
        preferred_element_type=jnp.float32,
    )
    cover = lax.psum(partial_cover, ("rowa", "rowb", "col"))
    previous = vectors
    lower = None
    for step in range(STEPS):
        previous = vectors
        products = jnp.dot(vectors, cover, precision=high, preferred_element_type=jnp.float32)
        vectors, lower = normalize(outer_gram(products), products)
    images = apply_rows(previous, regrouped)
    left = gather_directly(images, "col", 1)
    return (own_columns(vectors, start), left, jnp.diagonal(lower) / rows_total)


def solution(mesh):
    placed = (P(("rowa", "rowb"), "col"), P(None, "col"))
    return jax.shard_map(
        on_device,
        mesh=mesh,
        in_specs=placed,
        out_specs=(P(None, "col"), P(None, ("rowa", "rowb")), P()),
        check_vma=False,
    )
```

profile of v0, /device:TPU:1, one launch (start us, length us, event | category | flops | bytes accessed | tf_op | source)
XLA Modules:
  0.0 292.2 jit_solution(9501686616633930515)
XLA Ops:
  7.2 54.2 %all_to_all.29 = f32[4,2048,128]{2,1,0:T(8,128)} all-to-all(f32[4,2048,128]{2,1,0:T(8,128)} %bitcast.136), channel_id=1, replica_groups=mesh['rowa'=2,'rowb'=16,'col'=4] {'col'}, dimensions={0} | all-to-all | bytes 8388608 | tf_op jit(solution)/shard_map/all_to_all | solution.py:55
  61.4 5.4 %copy.40 = f32[2048,4,128]{0,2,1:T(8,128)} copy(f32[2048,4,128]{2,0,1:T(8,128)} %bitcast.135) | data formatting | bytes 8388608 | tf_op jit(solution)/shard_map/all_to_all | solution.py:55
  66.8 10.3 %fusion.51 = f32[512,512]{1,0:T(8,128)} fusion(f32[2048,512]{0,1:T(8,128)} %bitcast.133), kind=kOutput, calls=%fused_computation.81 | convolution fusion | flops 6442450944 | bytes 5242880 | tf_op jit(solution)/shard_map/dot_general | solution.py:58
  77.8 4.3 %all-to-all-start.1 = ((f32[4,16,128]{2,1,0:T(8,128)}), f32[4,16,128]{2,1,0:T(8,128)S(1)}, u32[]{:S(2)}, u32[]{:S(2)}) async-start(f32[4,16,128]{2,1,0:T(8,128)} %broadcast_in_dim.7), calls=%async_computation.1 | async-start | bytes 65536 | tf_op jit(solution)/shard_map/all_to_all | solution.py:20
  82.0 3.2 %all-to-all-done.1 = f32[4,16,128]{2,1,0:T(8,128)S(1)} async-done(((f32[4,16,128]{2,1,0:T(8,128)}), f32[4,16,128]{2,1,0:T(8,128)S(1)}, u32[]{:S(2)}, u32[]{:S(2)}) %all-to-all-start.1) | async-done | bytes 32800 | tf_op jit(solution)/shard_map/all_to_all | solution.py:20
  85.2 143.2 %all-reduce.2.cloned.1.call-done = f32[512,512]{1,0:T(8,128)} async-done(((f32[512,512]{1,0:T(8,128)}), f32[512,512]{1,0:T(8,128)}) %all-reduce.2.cloned.1.call-update) | async-done | bytes 1048592 | tf_op jit(solution)/shard_map/psum | solution.py:65
  228.4 2.0 fusion
  230.6 1.5 cholesky.134
  233.5 1.2 custom-call.14
  234.9 1.9 fusion.53
  237.0 1.5 cholesky.145
  239.8 1.2 custom-call.15
  241.3 1.9 fusion.55
  243.4 1.5 cholesky.156
  246.2 1.2 custom-call.16
  248.5 1.5 cholesky.167
  251.3 1.2 custom-call.17
  253.6 1.5 cholesky.178
  258.8 1.5 cholesky.189
  263.9 1.5 cholesky.200
  268.2 4.3 %fusion.67 = f32[16,2048]{1,0:T(8,128)S(1)} fusion(f32[16,512]{1,0:T(8,128)S(1)} %fusion.15, f32[2048,512]{0,1:T(8,128)} %bitcast.134), kind=kOutput, calls=%fused_computation.97 | convolution fusion | flops 201326592 | bytes 4358144 | tf_op jit(solution)/shard_map/dot_general | solution.py:28
  273.3 3.5 %all-to-all-start.2 = ((f32[4,16,2048]{2,1,0:T(8,128)}), f32[4,16,2048]{2,1,0:T(8,128)S(1)}, u32[]{:S(2)}, u32[]{:S(2)}) async-start(f32[4,16,2048]{2,1,0:T(8,128)} %broadcast_in_dim.8), calls=%async_computation.2 | async-start | bytes 1048576 | tf_op jit(solution)/shard_map/all_to_all | solution.py:20
  277.6 1.5 cholesky.211
  280.4 1.2 custom-call.21
  (78 shorter events, 26.1 us)
Async XLA Ops:
  7.2 221.3 %all-reduce.2.cloned.1.call-start = ((), (), s32[]{:S(2)}) async-start(), calls=%async_computation.3 | async-start | bytes 2097152 | tf_op jit(solution)/shard_map/psum | solution.py:65
  66.8 10.3 %copy-start.1 = (f32[16,128]{1,0:T(8,128)S(1)}, f32[16,128]{1,0:T(8,128)}, u32[]{:S(2)}) copy-start(f32[16,128]{1,0:T(8,128)} %param.6) | copy-start | bytes 24580
  77.8 7.4 %all-to-all-start.1 = ((f32[4,16,128]{2,1,0:T(8,128)}), f32[4,16,128]{2,1,0:T(8,128)S(1)}, u32[]{:S(2)}, u32[]{:S(2)}) async-start(f32[4,16,128]{2,1,0:T(8,128)} %broadcast_in_dim.7), calls=%async_computation.1 | async-start | bytes 65536 | tf_op jit(solution)/shard_map/all_to_all | solution.py:20
  228.4 19.2 %copy-start = (f32[512,512]{1,0:T(8,128)S(1)}, f32[512,512]{1,0:T(8,128)}, u32[]{:S(2)}) copy-start(f32[512,512]{1,0:T(8,128)} %all-reduce.2.cloned.1.call-done) | copy-start | bytes 3145732
  273.3 11.2 %all-to-all-start.2 = ((f32[4,16,2048]{2,1,0:T(8,128)}), f32[4,16,2048]{2,1,0:T(8,128)S(1)}, u32[]{:S(2)}, u32[]{:S(2)}) async-start(f32[4,16,2048]{2,1,0:T(8,128)} %broadcast_in_dim.8), calls=%async_computation.2 | async-start | bytes 1048576 | tf_op jit(solution)/shard_map/all_to_all | solution.py:20
Sparse Core Ops, SparseCore 0:
  77.2 151.1 all-reduce.1
where the time goes:
time: 293 us; the launch traced here: 292 us
  waiting for transfers between devices  147 us (50%)
  blocking collectives  54.2 us (18%)
  other arithmetic  32.8 us (11%)
  matrix products  26.4 us (9%)
  between operations  14.2 us (5%)
  local copies, waits for them, and re-layouts  9.6 us (3%)
  starting transfers between devices  7.77 us (3%)
    psum x1, waiting for transfers between devices, on_device(): cover = lax.psum(partial_cover, ('rowa', 'rowb', 'col'))  143 us
    all_to_all x1, blocking collectives, on_device(): lax.all_to_all(table, 'col', split_axis=0, concat_axis=1, tiled=True)  54.2 us
    another operation x24, other arithmetic, normalize(): lower = jnp.linalg.cholesky(gram)  17.2 us
    another operation x16, other arithmetic, normalize(): jax.scipy.linalg.solve_triangular(lower, products, lower=True)  15 us
    dot_general x1, matrix products, on_device(): lax.dot_general(regrouped, regrouped, (((0,), (0,)), ((), ())), precision...  10.3 us
    dot_general x8, matrix products, on_device(): jnp.dot(vectors, cover, precision=high, preferred_element_type=jnp.float32)  8.81 us
    all_to_all x2, starting transfers between devices, from_everyone(): lax.all_to_all(jnp.broadcast_to(x[None], (length, *x.shape)), axis, 0, 0,...  7.73 us
  transfers between devices with their start and end apart: 3, of which 3 were waited for; matrix products, arithmetic and copies ran while one was open for 3% of the time, Pallas kernels for 0%

commit v1 on v0

v1 whole, which is shorter than its diff:
```python
import functools

import jax
import jax.numpy as jnp
from jax import lax
from jax.experimental import pallas as pl
from jax.experimental.pallas import tpu as pltpu
from jax.sharding import PartitionSpec as P

STEPS = 8
MESH = pl.DeviceIdType.MESH
f32 = jnp.float32
bf16 = jnp.bfloat16
CHUNKS = 8
CW = 16


def dot(a, b):
    return lax.dot_general(a, b, (((1,), (0,)), ((), ())), preferred_element_type=f32)


def dot_nt(a, b):
    return lax.dot_general(a, b, (((1,), (1,)), ((), ())), preferred_element_type=f32)


def split2(x):
    h = x.astype(bf16)
    return h, (x - h.astype(f32)).astype(bf16)


def split3(x):
    h = x.astype(bf16)
    r = x - h.astype(f32)
    m = r.astype(bf16)
    return h, m, (r - m.astype(f32)).astype(bf16)


def times_cover(v, g1, g2, g3):
    h, m, l = split3(v)
    a = jnp.concatenate([h, m, l], 0)
    o1, o2, o3 = dot(a, g1[...]), dot(a[:32], g2[...]), dot(h, g3[...])
    return o1[:16] + (o1[16:32] + o2[:16]) + (o1[32:] + o2[16:] + o3)


def outer_gram(p):
    h, m, l = split3(p)
    a = jnp.concatenate([h, m, l], 0)
    o1, o2, o3 = dot_nt(a, h), dot_nt(a[:32], m), dot_nt(h, l)
    return o1[:16] + (o1[16:32] + o2[:16]) + (o1[32:] + o2[16:] + o3)


def orthonormal(gram, p):
    rows = lax.broadcasted_iota(jnp.int32, (16, 128), 0)
    cols = [jnp.broadcast_to(gram[:, k : k + 1], (16, 128)) for k in range(16)]
    tiles = [p[:, 128 * t : 128 * t + 128] for t in range(4)]
    pivots = jnp.zeros((16, 128), f32)
    for k in range(16):
        d = cols[k][k : k + 1, :]
        pivots = jnp.where(rows == k, d, pivots)
        if k < 15:
            m = jnp.where(rows > k, cols[k] * (1.0 / d), 0.0)
            for j in range(k + 1, 16):
                cols[j] = cols[j] - m * cols[j][k : k + 1, :]
            tiles = [t - m * t[k : k + 1, :] for t in tiles]
    s = jnp.sqrt(pivots)
    r = 1.0 / s
    return jnp.concatenate([t * r for t in tiles], 1), s


def kernel(
    rows_total,
    table, start, right_o, left_o, str_o,
    tab, tt, rt, stt, frt, wh, wl, ih, il, rst,
    src, ry, sy, rz, sx, rx, gz, gy,
    g1, g2, g3, img, limg, vs,
    load_s, st_s, st_r, nat_s, nat_r, tq_s, tq_r, ex_s, ex_r, fw_s, fw_r,
    y_s, y_r, z_s, z_r, x_s, x_r, az_s, az_r, ay_s, ay_r,
    im_s, im_r, if_s, if_r, out_s,
):
    ra, rb, c = lax.axis_index("rowa"), lax.axis_index("rowb"), lax.axis_index("col")
    y, z = rb % 4, rb // 4
    core, half = c % 2, c // 2
    mine, other = 2 * half, 2 - 2 * half
    sib, par, dia = c ^ 1, c ^ 2, c ^ 3

    def at_col(k):
        return (ra, rb, k)

    def at_y(d):
        return (ra, z * 4 + (y ^ d), c)

    def at_z(d):
        return (ra, (z ^ d) * 4 + y, c)

    def at_x(da, dc):
        return (ra ^ da, rb, c ^ dc)

    pending = []

    def send(a, b, s, r, dev):
        cp = pltpu.make_async_remote_copy(
            src_ref=a, dst_ref=b, send_sem=s, recv_sem=r, device_id=dev, device_id_type=MESH
        )
        cp.start()
        pending.append(cp)
        return cp

    XP = [(da, dc) for da in range(2) for dc in range(4) if (da, dc) != (0, 0)]

    loads = []
    for i, q in enumerate((other, other + 1, mine, mine + 1)):
        cp = pltpu.make_async_copy(table.at[pl.ds(q * 2048, 2048), :], tab.at[core, q], load_s.at[i])
        cp.start()
        loads.append(cp)

    barrier = pltpu.get_barrier_semaphore()
    for d in (1, 2, 3):
        pl.semaphore_signal(barrier, inc=1, device_id=at_y(d), device_id_type=MESH)
        pl.semaphore_signal(barrier, inc=1, device_id=at_z(d), device_id_type=MESH)
    for da, dc in XP:
        pl.semaphore_signal(barrier, inc=1, device_id=at_x(da, dc), device_id_type=MESH)

    def transpose_quarter(q):
        def body(i, carry):
            o = pl.multiple_of(i * 256, 256)
            tt[q, :, pl.ds(o, 256)] = tab[core, q, pl.ds(o, 256), :].T
            return carry

        lax.fori_loop(0, 8, body, 0)

    exchange = {}

    def send_chunk(j, k):
        w = pl.ds(CW * j, CW)
        exchange[j, k] = send(tt.at[other + k, w], rt.at[k, w], ex_s.at[j, k], ex_r.at[j, k], at_col(par))

    loads[0].wait()
    transpose_quarter(other)
    pl.semaphore_wait(barrier, 13)
    send_chunk(0, 0)
    nat = []
    for i, q in enumerate((mine, mine + 1, other, other + 1)):
        nat.append(
            send(table.at[pl.ds(q * 2048, 2048), :], tab.at[core, q], nat_s.at[i], nat_r.at[i], at_col(sib))
        )
    loads[1].wait()
    transpose_quarter(other + 1)
    for j, k in ((0, 1), (1, 0), (1, 1)):
        send_chunk(j, k)
    starts = [
        send(start, rst.at[c], st_s.at[d - 1], st_r.at[d - 1], at_col(c ^ d)) for d in (1, 2, 3)
    ]
    rst[c] = start[...]
    loads[2].wait()
    transpose_quarter(mine)
    loads[3].wait()
    transpose_quarter(mine + 1)
    tq = send(tt.at[mine + 1 - core], stt, tq_s, tq_r, at_col(sib))

    acc = jnp.zeros((128, 256), f32)
    for i, q in enumerate((mine, mine + 1, other, other + 1)):
        nat[i].wait_recv()

        def body(t, acc, i=i, q=q):
            o = pl.multiple_of(t * 512, 512)
            w = jnp.concatenate([tab[0, q, pl.ds(o, 512), :], tab[1, q, pl.ds(o, 512), :]], 1)
            h, l = split2(w)
            if i < 2:
                wh[i, pl.ds(o, 512), :] = h
                wl[i, pl.ds(o, 512), :] = l
            ah, al = split2(tt[q, :, pl.ds(o, 512)])
            both = dot(jnp.concatenate([ah, al], 0), h)
            return acc + (both[:128] + (both[128:] + dot(ah, l)))

        acc = lax.fori_loop(0, 4, body, acc)
    src[0] = acc.reshape(4, 32, 256)

    def split_rows(block, ref):
        def body(i, carry):
            o = pl.multiple_of(i * 512, 512)
            h, l = split2(ref[:, pl.ds(o, 512)])
            ih[block, :, pl.ds(o, 512)] = h
            il[block, :, pl.ds(o, 512)] = l
            return carry

        lax.fori_loop(0, 4, body, 0)

    cps = {}

    def stage0(s):
        cps["y", s] = [
            send(src.at[s, y ^ d], ry.at[s, d - 1], y_s.at[s, d - 1], y_r.at[s, d - 1], at_y(d)) for d in (1, 2, 3)
        ]

    def stage1(s):
        for cp in cps["y", s]:
            cp.wait_recv()
        sy[s] = (src[s, y] + ry[s, 0] + (ry[s, 1] + ry[s, 2])).reshape(4, 8, 256)
        cps["z", s] = [
            send(sy.at[s, z ^ d], rz.at[s, d - 1], z_s.at[s, d - 1], z_r.at[s, d - 1], at_z(d)) for d in (1, 2, 3)
        ]

    def stage2(s):
        for cp in cps["z", s]:
            cp.wait_recv()
        total = sy[s, z] + rz[s, 0] + (rz[s, 1] + rz[s, 2])
        sx[s] = total
        rx[s, ra, c] = total
        cps["x", s] = [
            send(sx.at[s], rx.at[s, ra, c], x_s.at[s, i], x_r.at[s, i], at_x(da, dc)) for i, (da, dc) in enumerate(XP)
        ]

    def stage3(s):
        for cp in cps["x", s]:
            cp.wait_recv()
        gz[s, z] = rx[s, 0] + rx[s, 1]
        cps["az", s] = [
            send(gz.at[s, z], gz.at[s, z], az_s.at[s, d - 1], az_r.at[s, d - 1], at_z(d)) for d in (1, 2, 3)
        ]

    def stage4(s):
        for cp in cps["az", s]:
            cp.wait_recv()
        cps["ay", s] = [
            send(gz.at[s], gy.at[s, y], ay_s.at[s, d - 1], ay_r.at[s, d - 1], at_y(d)) for d in (1, 2, 3)
        ]
        gy[s, y] = gz[s]

    def stage5(s):
        for cp in cps["ay", s]:
            cp.wait_recv()

    stage0(0)
    split_rows(c, tt.at[mine + core])
    tq.wait_recv()
    split_rows(sib, stt)

    forwards = []
    for j in range(CHUNKS):
        w = pl.ds(CW * j, CW)
        for k in range(2):
            exchange[j, k].wait_recv()
        if j + 2 < CHUNKS:
            for k in range(2):
                exchange[j, k].wait_send()
                pending[:] = [p for p in pending if p is not exchange[j, k]]
                send_chunk(j + 2, k)
        forwards.append(send(rt.at[1 - core, w], frt.at[w], fw_s.at[j], fw_r.at[j], at_col(sib)))
        total = jnp.zeros((CW, 256), f32)
        for k in range(2):

            def body(t, total, k=k, j=j):
                o = pl.multiple_of(t * 1024, 1024)
                ah, al = split2(rt[k, pl.ds(CW * j, CW), pl.ds(o, 1024)])
                h, l = wh[k, pl.ds(o, 1024), :], wl[k, pl.ds(o, 1024), :]
                both = dot(jnp.concatenate([ah, al], 0), h)
                return total + (both[:CW] + (both[CW:] + dot(ah, l)))

            total = lax.fori_loop(0, 2, body, total)
        src[1, CW * j // 32, pl.ds(CW * j % 32, CW), :] = total
        h, l = split2(rt[core, w, :])
        ih[par, w, :] = h
        il[par, w, :] = l
        if j == 1:
            stage1(0)
        if j == 2:
            stage2(0)
        if j == 5:
            stage3(0)
        if j == 6:
            stage4(0)
        if j == 7:
            stage0(1)
            stage5(0)
    for j in range(CHUNKS):
        forwards[j].wait_recv()
    split_rows(dia, frt)

    def block(s, k):
        return gy[s, :, :, k].reshape(128, 256)

    def store_cover(r, k, x):
        for ref, part in zip((g1, g2, g3), split3(x)):
            ref[r : r + 128, k : k + 256] = part

    store_cover(0, 0, block(0, 0))
    store_cover(128, 0, block(0, 1))
    store_cover(256, 256, block(0, 2))
    store_cover(384, 256, block(0, 3))
    for cp in starts:
        cp.wait_recv()
    vectors = jnp.concatenate([rst[k] for k in range(4)], 1)

    stage1(1)
    stage2(1)
    stage3(1)
    stage4(1)
    stage5(1)
    upper = jnp.concatenate([block(1, 2), block(1, 3)], 0)
    below = jnp.concatenate([block(1, 0), block(1, 1)], 0)
    upper = upper + below.T
    store_cover(0, 256, upper[:128])
    store_cover(128, 256, upper[128:])
    below = upper.T
    store_cover(256, 0, below[:128])
    store_cover(384, 0, below[128:])

    def step(vectors):
        products = times_cover(vectors, g1, g2, g3)
        return orthonormal(outer_gram(products), products)

    vectors = lax.fori_loop(0, STEPS - 1, lambda i, v: step(v)[0], vectors)

    vh, vl = split2(vectors)
    vb = jnp.concatenate([vh, vl], 0)
    images = []
    for n in range(2):
        for t in range(2):
            o = 1024 * n + 512 * t
            h = jnp.concatenate([ih[k, :, o : o + 512] for k in range(4)], 0)
            l = jnp.concatenate([il[k, :, o : o + 512] for k in range(4)], 0)
            both = dot(vb, h)
            part = both[:16] + (both[16:] + dot(vh, l))
            img[n, :, 512 * t : 512 * t + 512] = part
            limg[n, c, :, 512 * t : 512 * t + 512] = part
        images.append(
            [
                send(img.at[n], limg.at[n, c], im_s.at[n, i], im_r.at[n, i], at_col(k))
                for i, k in enumerate((par, sib))
            ]
        )
    vectors, diagonal = step(vectors)
    for k in range(4):
        vs[k] = vectors[:, 128 * k : 128 * k + 128]
    right_o[...] = vs[c]
    eye = lax.broadcasted_iota(jnp.int32, (16, 128), 0) == lax.broadcasted_iota(jnp.int32, (16, 128), 1)
    str_o[...] = jnp.sum(jnp.where(eye, diagonal / rows_total, 0.0), 0, keepdims=True)[:, :16]

    outs = []

    def put(n, k):
        cp = pltpu.make_async_copy(
            limg.at[n, k], left_o.at[:, pl.ds(pl.multiple_of(2048 * k + 1024 * n, 1024), 1024)], out_s.at[n, len(outs)]
        )
        cp.start()
        outs.append(cp)

    all_outs = []
    relays = []
    for n in range(2):
        outs = []
        put(n, c)
        images[n][1].wait_recv()
        put(n, sib)
        images[n][0].wait_recv()
        relays.append(send(limg.at[n, par], limg.at[n, par], if_s.at[n], if_r.at[n], at_col(sib)))
        put(n, par)
        all_outs.append(outs)
    for n in range(2):
        outs = all_outs[n]
        relays[n].wait_recv()
        put(n, dia)
    for cp in all_outs[0] + all_outs[1]:
        cp.wait()
    for cp in pending:
        cp.wait_send()


def on_device(rows_total, table, start):
    V, D = pltpu.VMEM, pltpu.SemaphoreType.DMA
    scratch = [
        V((2, 4, 2048, 128), f32),
        V((4, 128, 2048), f32),
        V((2, 128, 2048), f32),
        V((128, 2048), f32),
        V((128, 2048), f32),
        V((2, 2048, 256), bf16),
        V((2, 2048, 256), bf16),
        V((4, 128, 2048), bf16),
        V((4, 128, 2048), bf16),
        V((4, 16, 128), f32),
        V((2, 4, 32, 256), f32),
        V((2, 3, 32, 256), f32),
        V((2, 4, 8, 256), f32),
        V((2, 3, 8, 256), f32),
        V((2, 8, 256), f32),
        V((2, 2, 4, 8, 256), f32),
        V((2, 4, 4, 8, 256), f32),
        V((2, 4, 4, 4, 8, 256), f32),
        V((512, 512), bf16),
        V((512, 512), bf16),
        V((512, 512), bf16),
        V((2, 16, 1024), f32),
        V((2, 4, 16, 1024), f32),
        V((4, 16, 128), f32),
        D((4,)),
        D((3,)), D((3,)),
        D((4,)), D((4,)),
        D, D,
        D((CHUNKS, 2)), D((CHUNKS, 2)),
        D((CHUNKS,)), D((CHUNKS,)),
        D((2, 3)), D((2, 3)),
        D((2, 3)), D((2, 3)),
        D((2, 7)), D((2, 7)),
        D((2, 3)), D((2, 3)),
        D((2, 3)), D((2, 3)),
        D((2, 2)), D((2, 2)),
        D((2,)), D((2,)),
        D((2, 4)),
    ]
    right, left, strengths = pl.pallas_call(
        functools.partial(kernel, rows_total),
        out_shape=[
            jax.ShapeDtypeStruct((16, 128), f32),
            jax.ShapeDtypeStruct((16, 8192), f32),
            jax.ShapeDtypeStruct((1, 16), f32),
        ],
        in_specs=[pl.BlockSpec(memory_space=pl.ANY), pl.BlockSpec(memory_space=pltpu.VMEM)],
        out_specs=[
            pl.BlockSpec(memory_space=pltpu.VMEM),
            pl.BlockSpec(memory_space=pl.ANY),
            pl.BlockSpec(memory_space=pltpu.VMEM),
        ],
        scratch_shapes=scratch,
        compiler_params=pltpu.CompilerParams(
            collective_id=0, has_side_effects=True, vmem_limit_bytes=56 * 1024 * 1024
        ),
    )(table, start)
    return right, left, strengths.reshape(16)


def solution(mesh):
    rows_total = 8192 * mesh.shape["rowa"] * mesh.shape["rowb"]
    return jax.shard_map(
        functools.partial(on_device, rows_total),
        mesh=mesh,
        in_specs=(P(("rowa", "rowb"), "col"), P(None, "col")),
        out_specs=(P(None, "col"), P(None, ("rowa", "rowb")), P()),
        check_vma=False,
    )
```

time: 293 us -> 98.3 us (0.34)
  waiting for transfers between devices: 147 us -> 0 us
  Pallas kernels: 0 us -> 93.1 us
  blocking collectives: 54.2 us -> 0 us
  other arithmetic: 32.8 us -> 0 us
  matrix products: 26.4 us -> 0 us
  between operations: 14.2 us -> 0.64 us
  starting transfers between devices: 7.77 us -> 0 us
  local copies, waits for them, and re-layouts: 9.6 us -> 4.34 us
    psum x1 -> x0, waiting for transfers between devices: 143 us -> none  [on_device(): cover = lax.psum(partial_cover, ('rowa', 'rowb', 'col'))]
    pallas_call x0 -> x1, Pallas kernels: none -> 93.1 us  [on_device(): pl.pallas_call(functools.partial(kernel, rows_total), out_shape=[jax.Shap...]
    all_to_all x1 -> x0, blocking collectives: 54.2 us -> none  [on_device(): lax.all_to_all(table, 'col', split_axis=0, concat_axis=1, tiled=True)]
    another operation x40 -> x0, other arithmetic: 32.2 us -> none  [the longest x24 17.2 us: normalize(): lower = jnp.linalg.cholesky(gram)]
    dot_general x18 -> x0, matrix products: 24.6 us -> none  [the longest x1 10.3 us: on_device(): lax.dot_general(regrouped, regrouped, (((0,), (0,)), ((), ())), precision...]
    all_to_all x2 -> x0, starting transfers between devices: 7.73 us -> none  [from_everyone(): lax.all_to_all(jnp.broadcast_to(x[None], (length, *x.shape)), axis, 0, 0,...]
    all_to_all x1 -> x0, local copies, waits for them, and re-layouts: 5.37 us -> none  [on_device(): lax.all_to_all(table, 'col', split_axis=0, concat_axis=1, tiled=True)]
    unnamed x4 -> x3, local copies, waits for them, and re-layouts: 0.02 us -> 4.34 us
  transfers between devices with their start and end apart: 3 -> 0, of which waited for: 3 -> 0; matrix products, arithmetic and copies ran while one was open for 3% -> 0% of each run, Pallas kernels for 0% -> 0%
where the time goes in v1:
time: 98.3 us; the launch traced here: 98.1 us
  Pallas kernels  93.1 us (95%)
  local copies, waits for them, and re-layouts  4.34 us (4%)
    pallas_call x1, Pallas kernels, on_device(): pl.pallas_call(functools.partial(kernel, rows_total), out_shape=[jax.Shap...  93.1 us
    unnamed x3, local copies, waits for them, and re-layouts  4.34 us

profile of v1, /device:TPU:1, one launch (start us, length us, event | category | flops | bytes accessed | tf_op | source)
XLA Modules:
  0.0 98.1 jit_solution(8818805284617022617)
XLA Ops:
  0.6 93.1 %shard_map.49 = (f32[16,128]{1,0:T(8,128)}, f32[16,8192]{1,0:T(8,128)}, f32[1,16]{1,0:T(1,128)}) custom-call(f32[8192,128]{1,0:T(8,128)} %table.1, f32[16,128]{1,0:T(8,128)} %start.1), custom_call_target="tpu_custom_call" | custom-call | tf_op jit(solution)/shard_map/pallas_call | solution.py:411
  93.7 1.3 %copy.8 = f32[16,128]{1,0:T(8,128)} copy(f32[16,128]{1,0:T(8,128)} %get-tuple-element.12) | data formatting | bytes 16384
  95.0 1.9 %copy.9 = f32[16,8192]{1,0:T(8,128)} copy(f32[16,8192]{1,0:T(8,128)} %get-tuple-element.13) | data formatting | bytes 1048576
  96.9 1.2 %copy.10 = f32[16]{0:T(128)} copy(f32[16]{0:T(128)} %bitcast.1) | data formatting | bytes 128

commit v2 on v1

v2 whole, which is shorter than its diff:
```python
import functools

import jax
import jax.numpy as jnp
from jax import lax
from jax.experimental import pallas as pl
from jax.experimental.pallas import tpu as pltpu
from jax.sharding import PartitionSpec as P

STEPS = 8
MESH = pl.DeviceIdType.MESH
f32 = jnp.float32
bf16 = jnp.bfloat16
CHUNKS = 8
CW = 16
PIECES = 4
IW = 2048 // PIECES


def dot(a, b):
    return lax.dot_general(a, b, (((1,), (0,)), ((), ())), preferred_element_type=f32)


def dot_nt(a, b):
    return lax.dot_general(a, b, (((1,), (1,)), ((), ())), preferred_element_type=f32)


def split2(x):
    h = x.astype(bf16)
    return h, (x - h.astype(f32)).astype(bf16)


def split3(x):
    h = x.astype(bf16)
    r = x - h.astype(f32)
    m = r.astype(bf16)
    return h, m, (r - m.astype(f32)).astype(bf16)


def times_cover(v, g1, g2, g3):
    h, m, l = split3(v)
    a = jnp.concatenate([h, m, l], 0)
    o1, o2, o3 = dot(a, g1[...]), dot(a[:32], g2[...]), dot(h, g3[...])
    return o1[:16] + (o1[16:32] + o2[:16]) + (o1[32:] + o2[16:] + o3)


def outer_gram(p):
    h, m, l = split3(p)
    a = jnp.concatenate([h, m, l], 0)
    o1, o2, o3 = dot_nt(a, h), dot_nt(a[:32], m), dot_nt(h, l)
    return o1[:16] + (o1[16:32] + o2[:16]) + (o1[32:] + o2[16:] + o3)


def orthonormal(gram, p):
    rows = lax.broadcasted_iota(jnp.int32, (16, 128), 0)
    cols = [jnp.broadcast_to(gram[:, k : k + 1], (16, 128)) for k in range(16)]
    tiles = [p[:, 128 * t : 128 * t + 128] for t in range(4)]
    pivots = jnp.zeros((16, 128), f32)
    for k in range(16):
        d = cols[k][k : k + 1, :]
        pivots = jnp.where(rows == k, d, pivots)
        if k < 15:
            m = jnp.where(rows > k, cols[k] * (1.0 / d), 0.0)
            for j in range(k + 1, 16):
                cols[j] = cols[j] - m * cols[j][k : k + 1, :]
            tiles = [t - m * t[k : k + 1, :] for t in tiles]
    s = jnp.sqrt(pivots)
    r = 1.0 / s
    return jnp.concatenate([t * r for t in tiles], 1), s


def kernel(
    rows_total,
    table, start, right_o, left_o, str_o,
    tab, tt, rt, stt, frt, wh, wl, ih, il, rst,
    d_src, d_ry, d_sy, d_rz, d_sx, d_rx, d_gz, d_gy,
    e_src, e_ry, e_sy, e_rz, e_sx, e_rx, e_gz, e_gy,
    f_src, f_ry, f_sy, f_rz, f_sx, f_rx, f_gz, f_gy,
    t_src, t_ry, t_sy, t_rz, t_sx, t_rx, xg,
    g1, g2, g3, img, limg, vs,
    load_s, st_l, st_s, st_r, nat_s, nat_r, tq_s, tq_r, ex_s, ex_r, e0_s, e0_r, fw_s, fw_r,
    y_s, y_r, z_s, z_r, x_s, x_r, az_s, az_r, ay_s, ay_r,
    im_s, im_r, if_s, if_r,
):
    ra, rb, c = lax.axis_index("rowa"), lax.axis_index("rowb"), lax.axis_index("col")
    y, z = rb % 4, rb // 4
    core, half = c % 2, c // 2
    mine, other = 2 * half, 2 - 2 * half
    sib, par, dia = c ^ 1, c ^ 2, c ^ 3

    def at_col(k):
        return (ra, rb, k)

    def at_y(d):
        return (ra, z * 4 + (y ^ d), c)

    def at_z(d):
        return (ra, (z ^ d) * 4 + y, c)

    def at_x(da, dc):
        return (ra ^ da, rb, c ^ dc)

    pending = []

    def send(a, b, s, r, dev):
        cp = pltpu.make_async_remote_copy(
            src_ref=a, dst_ref=b, send_sem=s, recv_sem=r, device_id=dev, device_id_type=MESH
        )
        cp.start()
        pending.append(cp)
        return cp

    XP = [(da, dc) for da in range(2) for dc in range(4) if (da, dc) != (0, 0)]

    own_start = pltpu.make_async_copy(start, rst.at[c], st_l)

    def load(i, q, o, n):
        cp = pltpu.make_async_copy(
            table.at[pl.ds(q * 2048 + o, n), :], tab.at[core, q, pl.ds(o, n), :], load_s.at[i]
        )
        cp.start()
        return cp

    loads = [load(p, other, 512 * p, 512) for p in range(4)]
    loads += [load(4 + i, q, 0, 2048) for i, q in enumerate((other + 1, mine, mine + 1))]
    own_start.start()

    barrier = pltpu.get_barrier_semaphore()
    for d in (1, 2, 3):
        pl.semaphore_signal(barrier, inc=1, device_id=at_y(d), device_id_type=MESH)
        pl.semaphore_signal(barrier, inc=1, device_id=at_z(d), device_id_type=MESH)
    for da, dc in XP:
        pl.semaphore_signal(barrier, inc=1, device_id=at_x(da, dc), device_id_type=MESH)

    def transpose_rows(q, first, blocks):
        def body(i, carry):
            o = pl.multiple_of(first + i * 256, 256)
            tt[q, :, pl.ds(o, 256)] = tab[core, q, pl.ds(o, 256), :].T
            return carry

        lax.fori_loop(0, blocks, body, 0)

    exchange = {}

    def send_chunk(j, k):
        w = pl.ds(CW * j, CW)
        exchange[j, k] = [send(tt.at[other + k, w], rt.at[k, w], ex_s.at[j, k], ex_r.at[j, k], at_col(par))]

    exchange[0, 0] = []
    for p in range(4):
        loads[p].wait()
        transpose_rows(other, 512 * p, 2)
        if p == 0:
            pl.semaphore_wait(barrier, 13)
        o = pl.ds(512 * p, 512)
        exchange[0, 0].append(
            send(tt.at[other, :CW, o], rt.at[0, :CW, o], e0_s.at[p], e0_r.at[p], at_col(par))
        )
    nat = []
    for i, q in enumerate((mine, mine + 1, other, other + 1)):
        nat.append(
            send(table.at[pl.ds(q * 2048, 2048), :], tab.at[core, q], nat_s.at[i], nat_r.at[i], at_col(sib))
        )
    loads[4].wait()
    transpose_rows(other + 1, 0, 8)
    for j, k in ((0, 1), (1, 0), (1, 1)):
        send_chunk(j, k)
    own_start.wait()
    starts = [
        send(rst.at[c], rst.at[c], st_s.at[d - 1], st_r.at[d - 1], at_col(c ^ d)) for d in (1, 2, 3)
    ]
    loads[5].wait()
    transpose_rows(mine, 0, 8)
    loads[6].wait()
    transpose_rows(mine + 1, 0, 8)
    tq = send(tt.at[mine + 1 - core], stt, tq_s, tq_r, at_col(sib))

    acc = jnp.zeros((128, 256), f32)
    for i, q in enumerate((mine, mine + 1, other, other + 1)):
        nat[i].wait_recv()

        def body(t, acc, i=i, q=q):
            o = pl.multiple_of(t * 512, 512)
            w = jnp.concatenate([tab[0, q, pl.ds(o, 512), :], tab[1, q, pl.ds(o, 512), :]], 1)
            h, l = split2(w)
            if i < 2:
                wh[i, pl.ds(o, 512), :] = h
                wl[i, pl.ds(o, 512), :] = l
            ah, al = split2(tt[q, :, pl.ds(o, 512)])
            both = dot(jnp.concatenate([ah, al], 0), h)
            return acc + (both[:128] + (both[128:] + dot(ah, l)))

        acc = lax.fori_loop(0, 4, body, acc)
    d_src[...] = acc.reshape(4, 4, 8, 256)

    def split_rows(block, ref):
        def body(i, carry):
            o = pl.multiple_of(i * 512, 512)
            h, l = split2(ref[:, pl.ds(o, 512)])
            ih[block, :, pl.ds(o, 512)] = h
            il[block, :, pl.ds(o, 512)] = l
            return carry

        lax.fori_loop(0, 4, body, 0)

    def sends(pairs, s, r, devs):
        return [send(a, b, s.at[i], r.at[i], dev) for i, ((a, b), dev) in enumerate(zip(pairs, devs))]

    def arrived(copies):
        for cp in copies:
            cp.wait_recv()

    ys, zs = [at_y(d) for d in (1, 2, 3)], [at_z(d) for d in (1, 2, 3)]
    xs = [at_x(da, dc) for da, dc in XP]

    def scattered(g, src, ry, sy, rz, sx, rx, gz, gy):
        hold = {}

        def stage0():
            hold["y"] = sends([(src.at[y ^ d], ry.at[d - 1]) for d in (1, 2, 3)], y_s.at[g], y_r.at[g], ys)

        def stage1():
            arrived(hold["y"])
            sy[...] = src[y] + ry[0] + (ry[1] + ry[2])
            hold["z"] = sends([(sy.at[z ^ d], rz.at[d - 1]) for d in (1, 2, 3)], z_s.at[g], z_r.at[g], zs)

        def stage2():
            arrived(hold["z"])
            total = sy[z] + rz[0] + (rz[1] + rz[2])
            sx[...] = total
            rx[ra, c] = total
            hold["x"] = sends([(sx, rx.at[ra, c])] * 7, x_s.at[g], x_r.at[g], xs)

        def stage3():
            arrived(hold["x"])
            gz[z] = rx[0] + rx[1]
            hold["az"] = sends([(gz.at[z], gz.at[z])] * 3, az_s.at[g], az_r.at[g], zs)

        def stage4():
            arrived(hold["az"])
            hold["ay"] = sends([(gz, gy.at[y])] * 3, ay_s.at[g], ay_r.at[g], ys)
            gy[y] = gz[...]

        def stage5():
            arrived(hold["ay"])

        return stage0, stage1, stage2, stage3, stage4, stage5

    D = scattered(0, d_src, d_ry, d_sy, d_rz, d_sx, d_rx, d_gz, d_gy)
    E = scattered(1, e_src, e_ry, e_sy, e_rz, e_sx, e_rx, e_gz, e_gy)

    def f0():
        return sends([(f_src.at[y ^ d], f_ry.at[d - 1]) for d in (1, 2, 3)], y_s.at[2], y_r.at[2], ys)

    def f1(cps):
        arrived(cps)
        total = f_src[y] + f_ry[0] + (f_ry[1] + f_ry[2])
        f_sy[...] = total
        f_rz[z] = total
        return sends([(f_sy, f_rz.at[z])] * 3, z_s.at[2], z_r.at[2], zs)

    def f2(cps):
        arrived(cps)
        total = (f_rz[0] + f_rz[1]) + (f_rz[2] + f_rz[3])
        f_sx[...] = total
        f_rx[ra, c] = total
        return sends([(f_sx, f_rx.at[ra, c])] * 7, x_s.at[2], x_r.at[2], xs)

    def f3(cps):
        arrived(cps)
        f_gz[...] = f_rx[0] + f_rx[1]
        out = sends([(f_gz, f_gy.at[y])] * 3, ay_s.at[2], ay_r.at[2], ys)
        f_gy[y] = f_gz[...]
        return out

    def t0():
        t_ry[y] = t_src[...]
        return sends([(t_src, t_ry.at[y])] * 3, y_s.at[3], y_r.at[3], ys)

    def t1(cps):
        arrived(cps)
        total = (t_ry[0] + t_ry[1]) + (t_ry[2] + t_ry[3])
        t_sy[...] = total
        t_rz[z] = total
        return sends([(t_sy, t_rz.at[z])] * 3, z_s.at[3], z_r.at[3], zs)

    def t2(cps):
        arrived(cps)
        total = (t_rz[0] + t_rz[1]) + (t_rz[2] + t_rz[3])
        t_sx[...] = total
        t_rx[ra, c] = total
        return sends([(t_sx, t_rx.at[ra, c])] * 7, x_s.at[3], x_r.at[3], xs)

    D[0]()
    split_rows(c, tt.at[mine + core])
    tq.wait_recv()
    split_rows(sib, stt)

    def chunk_half(j, k, length):
        w = pl.ds(CW * j, CW)

        def body(t, total):
            o = pl.multiple_of(t * length, length)
            ah, al = split2(rt[k, w, pl.ds(o, length)])
            h, l = wh[k, pl.ds(o, length), :], wl[k, pl.ds(o, length), :]
            both = dot(jnp.concatenate([ah, al], 0), h)
            return total + (both[:CW] + (both[CW:] + dot(ah, l)))

        zero = jnp.zeros((CW, 256), f32)
        return body(0, zero) if length == 2048 else lax.fori_loop(0, 2048 // length, body, zero)

    def store_cover(r, k, x):
        for ref, part in zip((g1, g2, g3), split3(x)):
            ref[r : r + 128, k : k + 256] = part

    forwards = []
    for j in range(CHUNKS):
        w = pl.ds(CW * j, CW)
        last = j == CHUNKS - 1
        arrived(exchange[j, 0])
        total = chunk_half(j, 0, 1024)
        arrived(exchange[j, 1])
        if j == 2:
            D[2]()
        if j == 5:
            E[2]()
        if j + 2 < CHUNKS:
            for k in range(2):
                for cp in exchange[j, k]:
                    cp.wait_send()
                    pending[:] = [p for p in pending if p is not cp]
                send_chunk(j + 2, k)
        total = total + chunk_half(j, 1, 2048 if last else 1024)
        if j < 4:
            for i in range(2):
                for n in range(2):
                    e_src[j, 2 * i + n] = total[8 * i : 8 * i + 8, 128 * n : 128 * n + 128]
        elif j < 7:
            for i in range(2):
                for n in range(2):
                    u = (2 * (j - 4) + i) * 2 + n
                    f_src[u // 3, u % 3] = total[8 * i : 8 * i + 8, 128 * n : 128 * n + 128]
        else:
            t_src[...] = total
            tail = t0()
        forwards.append(send(rt.at[1 - core, w], frt.at[w], fw_s.at[j], fw_r.at[j], at_col(sib)))
        h, l = split2(rt[core, w, :])
        ih[par, w, :] = h
        il[par, w, :] = l
        if j == 1:
            D[1]()
        if j == 3:
            E[0]()
        if j == 4:
            D[3]()
            E[1]()
            D[4]()
        if j == 6:
            middle = f0()
            E[3]()
            D[5]()
            for k in range(4):
                store_cover(128 * k, 256 * (k // 2), d_gy[:, :, k].reshape(128, 256))
            E[4]()
            middle = f1(middle)
    middle = f2(middle)
    tail = t1(tail)
    middle = f3(middle)
    E[5]()
    for k in range(4):
        for t in range(4):
            for i in range(2):
                for n in range(2):
                    xg[k, 16 * t + 8 * i : 16 * t + 8 * i + 8, 128 * n : 128 * n + 128] = e_gy[t, 2 * i + n, k]
    tail = t2(tail)
    arrived(forwards)
    split_rows(dia, frt)
    arrived(starts)
    vectors = jnp.concatenate([rst[k] for k in range(4)], 1)
    arrived(middle)
    for k in range(4):
        for u in range(12):
            r = 64 + 8 * (u // 2)
            xg[k, r : r + 8, 128 * (u % 2) : 128 * (u % 2) + 128] = f_gy[u // 3, k, u % 3]
    arrived(tail)
    for k in range(4):
        xg[k, 112:128, :] = t_rx[0, k] + t_rx[1, k]
    upper = xg[2:4].reshape(256, 256) + xg[0:2].reshape(256, 256).T
    store_cover(0, 256, upper[:128])
    store_cover(128, 256, upper[128:])
    below = upper.T
    store_cover(256, 0, below[:128])
    store_cover(384, 0, below[128:])

    def step(vectors):
        products = times_cover(vectors, g1, g2, g3)
        return orthonormal(outer_gram(products), products)

    vectors = lax.fori_loop(0, STEPS - 1, lambda i, v: step(v)[0], vectors)

    vh, vl = split2(vectors)
    vb = jnp.concatenate([vh, vl], 0)
    images = []
    for n in range(PIECES):
        o = pl.ds(IW * n, IW)
        h = jnp.concatenate([ih[k, :, o] for k in range(4)], 0)
        l = jnp.concatenate([il[k, :, o] for k in range(4)], 0)
        both = dot(vb, h)
        part = both[:16] + (both[16:] + dot(vh, l))
        img[n] = part
        limg[n, c] = part
        images.append(
            [send(img.at[n], limg.at[n, c], im_s.at[n, i], im_r.at[n, i], at_col(k)) for i, k in enumerate((par, sib))]
        )
    vectors, diagonal = step(vectors)
    for k in range(4):
        vs[k] = vectors[:, 128 * k : 128 * k + 128]
    right_o[...] = vs[c]
    eye = lax.broadcasted_iota(jnp.int32, (16, 128), 0) == lax.broadcasted_iota(jnp.int32, (16, 128), 1)
    str_o[...] = jnp.sum(jnp.where(eye, diagonal / rows_total, 0.0), 0, keepdims=True)[:, :16]

    relays = []
    for n in range(PIECES):
        images[n][0].wait_recv()
        relays.append(send(limg.at[n, par], limg.at[n, par], if_s.at[n], if_r.at[n], at_col(sib)))
    for n in range(PIECES):
        images[n][1].wait_recv()
        relays[n].wait_recv()
        for k in range(4):
            left_o[:, 2048 * k + IW * n : 2048 * k + IW * n + IW] = limg[n, k]
    for cp in pending:
        cp.wait_send()


def write_out(a, b, d, ao, bo, do, sem):
    copies = [pltpu.make_async_copy(x, o, sem.at[i]) for i, (x, o) in enumerate(((a, ao), (b, bo), (d, do)))]
    for cp in copies:
        cp.start()
    for cp in copies:
        cp.wait()


def scattered_scratch(*unit):
    V = pltpu.VMEM
    return [
        V((4, 4, *unit), f32),
        V((3, 4, *unit), f32),
        V((4, *unit), f32),
        V((3, *unit), f32),
        V(unit, f32),
        V((2, 4, *unit), f32),
        V((4, 4, *unit), f32),
        V((4, 4, 4, *unit), f32),
    ]


def on_device(rows_total, table, start):
    V, D = pltpu.VMEM, pltpu.SemaphoreType.DMA
    scratch = [
        V((2, 4, 2048, 128), f32),
        V((4, 128, 2048), f32),
        V((2, 128, 2048), f32),
        V((128, 2048), f32),
        V((128, 2048), f32),
        V((2, 2048, 256), bf16),
        V((2, 2048, 256), bf16),
        V((4, 128, 2048), bf16),
        V((4, 128, 2048), bf16),
        V((4, 16, 128), f32),
        *scattered_scratch(8, 256),
        *scattered_scratch(8, 128),
        V((4, 3, 8, 128), f32),
        V((3, 3, 8, 128), f32),
        V((3, 8, 128), f32),
        V((4, 3, 8, 128), f32),
        V((3, 8, 128), f32),
        V((2, 4, 3, 8, 128), f32),
        V((4, 3, 8, 128), f32),
        V((4, 4, 3, 8, 128), f32),
        V((16, 256), f32),
        V((4, 16, 256), f32),
        V((16, 256), f32),
        V((4, 16, 256), f32),
        V((16, 256), f32),
        V((2, 4, 16, 256), f32),
        V((4, 128, 256), f32),
        V((512, 512), bf16),
        V((512, 512), bf16),
        V((512, 512), bf16),
        V((PIECES, 16, IW), f32),
        V((PIECES, 4, 16, IW), f32),
        V((4, 16, 128), f32),
        D((7,)),
        D, D((3,)), D((3,)),
        D((4,)), D((4,)),
        D, D,
        D((CHUNKS, 2)), D((CHUNKS, 2)),
        D((4,)), D((4,)),
        D((CHUNKS,)), D((CHUNKS,)),
        D((4, 3)), D((4, 3)),
        D((4, 3)), D((4, 3)),
        D((4, 7)), D((4, 7)),
        D((2, 3)), D((2, 3)),
        D((3, 3)), D((3, 3)),
        D((PIECES, 2)), D((PIECES, 2)),
        D((PIECES,)), D((PIECES,)),
    ]
    table, start = (pltpu.with_memory_space_constraint(x, pltpu.HBM) for x in (table, start))
    results = pl.pallas_call(
        functools.partial(kernel, rows_total),
        out_shape=[V((16, 128), f32), V((16, 8192), f32), V((1, 16), f32)],
        in_specs=[pl.BlockSpec(memory_space=pltpu.HBM)] * 2,
        out_specs=[pl.BlockSpec(memory_space=V)] * 3,
        scratch_shapes=scratch,
        compiler_params=pltpu.CompilerParams(
            collective_id=0, has_side_effects=True, vmem_limit_bytes=48 * 1024 * 1024
        ),
    )(table, start)
    right, left, strengths = pl.pallas_call(
        write_out,
        out_shape=[jax.ShapeDtypeStruct(x.shape, f32) for x in results],
        in_specs=[pl.BlockSpec(memory_space=V)] * 3,
        out_specs=[pl.BlockSpec(memory_space=pl.ANY)] * 3,
        scratch_shapes=[D((3,))],
        compiler_params=pltpu.CompilerParams(vmem_limit_bytes=1024 * 1024),
    )(*results)
    return right, left, strengths.reshape(16)


def solution(mesh):
    rows_total = 8192 * mesh.shape["rowa"] * mesh.shape["rowb"]
    return jax.shard_map(
        functools.partial(on_device, rows_total),
        mesh=mesh,
        in_specs=(P(("rowa", "rowb"), "col"), P(None, "col")),
        out_specs=(P(None, "col"), P(None, ("rowa", "rowb")), P()),
        check_vma=False,
    )
```

time: 98.3 us -> 84 us (0.85)
  Pallas kernels: 93.1 us -> 83.2 us
  local copies, waits for them, and re-layouts: 4.34 us -> 0 us
    pallas_call x1 -> x2, Pallas kernels: 93.1 us -> 83.2 us  [the longest x1 82.4 us: on_device(): pl.pallas_call(functools.partial(kernel, rows_total), out_shape=[V((16, 1...]
    unnamed x3 -> x0, local copies, waits for them, and re-layouts: 4.34 us -> none
where the time goes in v2:
time: 84 us; the launch traced here: 83.9 us
  Pallas kernels  83.2 us (99%)
    pallas_call x1, Pallas kernels, on_device(): pl.pallas_call(functools.partial(kernel, rows_total), out_shape=[V((16, 1...  82.4 us

profile of v2, /device:TPU:1, one launch (start us, length us, event | category | flops | bytes accessed | tf_op | source)
XLA Modules:
  0.0 83.9 jit_solution(6607955008785389955)
XLA Ops:
  0.6 82.4 %shard_map.49 = (f32[16,128]{1,0:T(8,128)S(1)}, f32[16,8192]{1,0:T(8,128)S(1)}, f32[1,16]{1,0:T(1,128)S(1)}) custom-call(f32[8192,128]{1,0:T(8,128)} %table.1, f32[16,128]{1,0:T(8,128)} %start.1), custom_call_target="tpu_custom_call" | custom-call | tf_op jit(solution)/shard_map/pallas_call | solution.py:509
  83.0 0.8 shard_map.50

commit v3 on v2

v3 whole, which is shorter than its diff:
```python
import functools
import math

import jax
import jax.numpy as jnp
from jax import lax
from jax.experimental import pallas as pl
from jax.experimental.pallas import tpu as pltpu
from jax.sharding import PartitionSpec as P

STEPS = 8
MESH = pl.DeviceIdType.MESH
f32 = jnp.float32
bf16 = jnp.bfloat16
WIDTHS = (16, 16, 16, 16, 16, 16, 16, 8, 8)
CHUNKS = len(WIDTHS)
PIECES = 8
IW = 2048 // PIECES


def dot(a, b):
    return lax.dot_general(a, b, (((1,), (0,)), ((), ())), preferred_element_type=f32)


def dot_nt(a, b):
    return lax.dot_general(a, b, (((1,), (1,)), ((), ())), preferred_element_type=f32)


def split2(x):
    h = x.astype(bf16)
    return h, (x - h.astype(f32)).astype(bf16)


def split3(x):
    h = x.astype(bf16)
    r = x - h.astype(f32)
    m = r.astype(bf16)
    return h, m, (r - m.astype(f32)).astype(bf16)


def times_cover(v, g1, g2, g3):
    h, m, l = split3(v)
    a = jnp.concatenate([h, m, l], 0)
    o1, o2, o3 = dot(a, g1[...]), dot(a[:32], g2[...]), dot(h, g3[...])
    return o1[:16] + (o1[16:32] + o2[:16]) + (o1[32:] + o2[16:] + o3)


def outer_gram(p):
    h, m, l = split3(p)
    a = jnp.concatenate([h, m, l], 0)
    o1, o2, o3 = dot_nt(a, h), dot_nt(a[:32], m), dot_nt(h, l)
    return o1[:16] + (o1[16:32] + o2[:16]) + (o1[32:] + o2[16:] + o3)


def orthonormal(gram, p):
    rows = lax.broadcasted_iota(jnp.int32, (16, 128), 0)
    cols = [jnp.broadcast_to(gram[:, k : k + 1], (16, 128)) for k in range(16)]
    tiles = [p[:, 128 * t : 128 * t + 128] for t in range(4)]
    pivots = jnp.zeros((16, 128), f32)
    for k in range(16):
        d = cols[k][k : k + 1, :]
        pivots = jnp.where(rows == k, d, pivots)
        if k < 15:
            m = jnp.where(rows > k, cols[k] * (1.0 / d), 0.0)
            for j in range(k + 1, 16):
                cols[j] = cols[j] - m * cols[j][k : k + 1, :]
            tiles = [t - m * t[k : k + 1, :] for t in tiles]
    s = jnp.sqrt(pivots)
    r = 1.0 / s
    return jnp.concatenate([t * r for t in tiles], 1), s


def kernel(
    rows_total,
    table, start, right_o, left_o, str_o,
    tab, tt, rt, stt, frt, wh, wl, ih, il, rst,
    d_src, d_ry, d_sy, d_rz, d_sx, d_rx, d_gz, d_gy,
    e_src, e_ry, e_sy, e_rz, e_sx, e_rx, e_gz, e_gy,
    f_src, f_ry, f_sy, f_rz, f_sx, f_rx, f_gz, f_gy,
    t_src, t_ry, t_sy, t_rz, t_sx, t_rx, xg,
    g1, g2, g3, img, limg, vs,
    load_s, st_l, st_r, nat_s, nat_r, tq_s, tq_r, ex_s, ex_r, fw_s, fw_r,
    all_s, y_r, z_r, x_r, az_r, ay_r, pair_r,
    im_s, im_r, if_s, if_r,
):
    ra, rb, c = lax.axis_index("rowa"), lax.axis_index("rowb"), lax.axis_index("col")
    y, z = rb % 4, rb // 4
    core, half = c % 2, c // 2
    mine, other = 2 * half, 2 - 2 * half
    sib, par, dia = c ^ 1, c ^ 2, c ^ 3

    def at_col(k):
        return (ra, rb, k)

    def at_y(d):
        return (ra, z * 4 + (y ^ d), c)

    def at_z(d):
        return (ra, (z ^ d) * 4 + y, c)

    def at_x(da, dc):
        return (ra ^ da, rb, c ^ dc)

    pending = []

    def send(a, b, s, r, dev):
        cp = pltpu.make_async_remote_copy(
            src_ref=a, dst_ref=b, send_sem=s, recv_sem=r, device_id=dev, device_id_type=MESH
        )
        cp.start()
        pending.append(cp)
        return cp

    def send_apart(*args):
        cp = send(*args)
        pending.pop()
        return cp

    class Waits:
        def __init__(self, whole, s, r):
            self.whole, self.s, self.r = whole, s, r

        def wait_send(self):
            pltpu.make_async_copy(self.whole, self.whole, self.s).wait()

        def wait_recv(self):
            pltpu.make_async_copy(self.whole, self.whole, self.r).wait()

    sent = [0]

    def sends(pairs, r, devs, whole):
        for (a, b), dev in zip(pairs, devs, strict=True):
            send_apart(a, b, all_s, r, dev)
        sent[0] += math.prod(whole.shape) // 1024
        return [Waits(whole, all_s, r)]

    three, seven = pl.ds(0, 3), pl.ds(0, 7)
    spot, spot2 = ra * 4 + c, ra * 2 + half
    pair = [at_col(sib)]

    def arrived(copies):
        for cp in copies:
            cp.wait_recv()

    XP = [(da, dc) for da in range(2) for dc in range(4) if (da, dc) != (0, 0)]

    own_start = pltpu.make_async_copy(start, rst.at[c], st_l)

    def load(i, q, o, n):
        cp = pltpu.make_async_copy(
            table.at[pl.ds(q * 2048 + o, n), :], tab.at[core, q, pl.ds(o, n), :], load_s.at[i]
        )
        cp.start()
        return cp

    loads = [load(p, other, 512 * p, 512) for p in range(4)]
    loads += [load(4 + i, q, 0, 2048) for i, q in enumerate((other + 1, mine, mine + 1))]
    own_start.start()

    barrier = pltpu.get_barrier_semaphore()
    for d in (1, 2, 3):
        pl.semaphore_signal(barrier, inc=1, device_id=at_y(d), device_id_type=MESH)
        pl.semaphore_signal(barrier, inc=1, device_id=at_z(d), device_id_type=MESH)
    for da, dc in XP:
        pl.semaphore_signal(barrier, inc=1, device_id=at_x(da, dc), device_id_type=MESH)

    def transpose_rows(q, first, blocks):
        def body(i, carry):
            o = pl.multiple_of(first + i * 256, 256)
            tt[q, :, pl.ds(o, 256)] = tab[core, q, pl.ds(o, 256), :].T
            return carry

        lax.fori_loop(0, blocks, body, 0)

    def columns(j):
        return pl.ds(sum(WIDTHS[:j]), WIDTHS[j])

    exchange = {}

    def send_chunk(j, k):
        w = columns(j)
        if (j, k) == (CHUNKS - 1, 1):
            halves = [(ex_s, ex_r.at[j + i, k], pl.ds(1024 * i, 1024)) for i in range(2)]
            exchange[j, k] = [
                send_apart(tt.at[other + k, w, o], rt.at[k, w, o], s, r, at_col(par)) for s, r, o in halves
            ]
            return
        exchange[j, k] = [send_apart(tt.at[other + k, w], rt.at[k, w], ex_s, ex_r.at[j, k], at_col(par))]

    for p in range(4):
        loads[p].wait()
        transpose_rows(other, 512 * p, 2)
        if p == 0:
            pl.semaphore_wait(barrier, 13)
        o = pl.ds(512 * p, 512)
        send_apart(tt.at[other, columns(0), o], rt.at[0, columns(0), o], ex_s, ex_r.at[0, 0], at_col(par))
    whole = rt.at[0, columns(0)]
    exchange[0, 0] = [Waits(whole, ex_s, ex_r.at[0, 0])]
    nat = []
    for i, q in enumerate((mine, mine + 1, other, other + 1)):
        nat.append(
            send_apart(table.at[pl.ds(q * 2048, 2048), :], tab.at[core, q], nat_s, nat_r.at[i], at_col(sib))
        )
    pending.append(Waits(tab.at[0], nat_s, nat_s))
    loads[4].wait()
    transpose_rows(other + 1, 0, 8)
    for j, k in ((0, 1), (1, 0), (1, 1)):
        send_chunk(j, k)
    own_start.wait()
    starts = sends([(rst.at[c], rst.at[c])] * 3, st_r, [at_col(c ^ d) for d in (1, 2, 3)], rst.at[three])
    loads[5].wait()
    transpose_rows(mine, 0, 8)
    loads[6].wait()
    transpose_rows(mine + 1, 0, 8)
    tq = send(tt.at[mine + 1 - core], stt, tq_s, tq_r, at_col(sib))

    acc = jnp.zeros((128, 256), f32)
    for i, q in enumerate((mine, mine + 1, other, other + 1)):
        nat[i].wait_recv()

        def body(t, acc, i=i, q=q):
            o = pl.multiple_of(t * 512, 512)
            w = jnp.concatenate([tab[0, q, pl.ds(o, 512), :], tab[1, q, pl.ds(o, 512), :]], 1)
            h, l = split2(w)
            if i < 2:
                wh[i, pl.ds(o, 512), :] = h
                wl[i, pl.ds(o, 512), :] = l
            ah, al = split2(tt[q, :, pl.ds(o, 512)])
            both = dot(jnp.concatenate([ah, al], 0), h)
            return acc + (both[:128] + (both[128:] + dot(ah, l)))

        acc = lax.fori_loop(0, 4, body, acc)
    d_src[...] = acc.reshape(4, 4, 8, 256)

    def split_rows(block, ref):
        def body(i, carry):
            o = pl.multiple_of(i * 512, 512)
            h, l = split2(ref[:, pl.ds(o, 512)])
            ih[block, :, pl.ds(o, 512)] = h
            il[block, :, pl.ds(o, 512)] = l
            return carry

        lax.fori_loop(0, 4, body, 0)

    ys, zs = [at_y(d) for d in (1, 2, 3)], [at_z(d) for d in (1, 2, 3)]
    xs = [at_x(da, dc) for da, dc in XP]
    xs2 = [at_x(da, dc) for da, dc in ((0, 2), (1, 0), (1, 2))]

    def scattered(g, src, ry, sy, rz, sx, rx, gz, gy):
        hold = {}

        def stage0():
            hold["y"] = sends([(src.at[y ^ d], ry.at[d - 1]) for d in (1, 2, 3)], y_r.at[g], ys, ry)

        def stage1():
            arrived(hold["y"])
            sy[...] = src[y] + ry[0] + (ry[1] + ry[2])
            hold["z"] = sends([(sy.at[z ^ d], rz.at[d - 1]) for d in (1, 2, 3)], z_r.at[g], zs, rz)

        def stage2():
            arrived(hold["z"])
            total = sy[z] + rz[0] + (rz[1] + rz[2])
            sx[...] = total
            rx[spot2] = total
            hold["x"] = sends([(sx, rx.at[spot2])] * 3, x_r.at[g], xs2, rx.at[three])

        def stage3():
            arrived(hold["x"])
            gz[z] = rx[:2] + rx[2:]
            hold["az"] = sends([(gz.at[z], gz.at[z])] * 3, az_r.at[g], zs, gz.at[three])

        def stage4():
            arrived(hold["az"])
            hold["ay"] = sends([(gz, gy.at[core, y])] * 3, ay_r.at[g], ys, gy.at[core, three])
            gy[core, y] = gz[...]

        def stage5():
            arrived(hold["ay"])
            hold["pair"] = sends([(gy.at[core], gy.at[core])], pair_r.at[g], pair, gy.at[core])

        def stage6():
            arrived(hold["pair"])

        return stage0, stage1, stage2, stage3, stage4, stage5, stage6

    D = scattered(0, d_src, d_ry, d_sy, d_rz, d_sx, d_rx, d_gz, d_gy)
    E = scattered(1, e_src, e_ry, e_sy, e_rz, e_sx, e_rx, e_gz, e_gy)

    def f0(i):
        return sends([(f_src.at[i, y ^ d], f_ry.at[i, d - 1]) for d in (1, 2, 3)], y_r.at[2 + i], ys, f_ry.at[i])

    def f1(i, cps):
        arrived(cps)
        total = f_src[i, y] + f_ry[i, 0] + (f_ry[i, 1] + f_ry[i, 2])
        f_sy[i] = total
        f_rz[i, z] = total
        return sends([(f_sy.at[i], f_rz.at[i, z])] * 3, z_r.at[2 + i], zs, f_rz.at[i, three])

    def f2(i, cps):
        arrived(cps)
        total = (f_rz[i, 0] + f_rz[i, 1]) + (f_rz[i, 2] + f_rz[i, 3])
        f_sx[i] = total
        f_rx[i, spot2] = total
        return sends([(f_sx.at[i], f_rx.at[i, spot2])] * 3, x_r.at[2 + i], xs2, f_rx.at[i, three])

    def f3(i, cps):
        arrived(cps)
        f_gz[i] = f_rx[i, :2] + f_rx[i, 2:]
        out = sends([(f_gz.at[i], f_gy.at[i, core, y])] * 3, ay_r.at[2 + i], ys, f_gy.at[i, core, three])
        f_gy[i, core, y] = f_gz[i]
        return out

    def f4(i, cps):
        arrived(cps)
        whole = f_gy.at[i, core]
        return sends([(whole, whole)], pair_r.at[2 + i], pair, whole)

    def t0(i):
        t_ry[i, y] = t_src[i]
        return sends([(t_src.at[i], t_ry.at[i, y])] * 3, y_r.at[5 + i], ys, t_ry.at[i, three])

    def t1(i, cps):
        arrived(cps)
        total = (t_ry[i, 0] + t_ry[i, 1]) + (t_ry[i, 2] + t_ry[i, 3])
        t_sy[i] = total
        t_rz[i, z] = total
        return sends([(t_sy.at[i], t_rz.at[i, z])] * 3, z_r.at[5 + i], zs, t_rz.at[i, three])

    def t2(i, cps):
        arrived(cps)
        total = (t_rz[i, 0] + t_rz[i, 1]) + (t_rz[i, 2] + t_rz[i, 3])
        t_sx[i] = total
        t_rx[i, spot] = total
        return sends([(t_sx.at[i], t_rx.at[i, spot])] * 7, x_r.at[5 + i], xs, t_rx.at[i, seven])

    D[0]()
    split_rows(c, tt.at[mine + core])
    tq.wait_recv()
    split_rows(sib, stt)

    def chunk_part(j, k, first, count):
        w, n = columns(j), WIDTHS[j]

        def body(t, total):
            o = pl.multiple_of(first + t * 1024, 1024)
            x = rt[k, w, pl.ds(o, 1024)]
            h = x.astype(bf16).astype(f32)
            both = jnp.concatenate([h, x - h], 0).astype(bf16)
            a, b = dot(both, wh[k, pl.ds(o, 1024), :]), dot(both, wl[k, pl.ds(o, 1024), :])
            return total + (a[:n] + ((a[n:] + b[:n]) + b[n:]))

        zero = jnp.zeros((n, 256), f32)
        return body(0, zero) if count == 1 else lax.fori_loop(0, count, body, zero)

    def store_cover(r, k, x):
        for ref, part in zip((g1, g2, g3), split3(x)):
            ref[r : r + 128, k : k + 256] = part

    def issue(i):
        if i < 2 * CHUNKS:
            send_chunk(i // 2, i % 2)

    f, t = {}, {}
    for j in range(CHUNKS):
        w = columns(j)
        last = j == CHUNKS - 1
        arrived(exchange[j, 0])
        total = chunk_part(j, 0, 0, 2)
        if j == 5:
            E[2]()
        if last:
            arrived(exchange[j, 1][:1])
            total = total + chunk_part(j, 1, 0, 1)
            f[2] = f1(2, f[2])
            arrived(exchange[j, 1][1:])
            total = total + chunk_part(j, 1, 1024, 1)
        else:
            arrived(exchange[j, 1])
        if j == 2:
            D[2]()
        if j == 6:
            f[0] = f2(0, f[0])
        for k in range(2):
            issue(2 * j + 4 + k)
        if not last:
            total = total + chunk_part(j, 1, 0, 2)
        if j < 7:
            for i in range(2):
                for n in range(2):
                    unit = total[8 * i : 8 * i + 8, 128 * n : 128 * n + 128]
                    if j < 4:
                        e_src[j, 2 * i + n] = unit
                    else:
                        f_src[j - 4, 2 * i + n] = unit
            if j >= 4:
                f[j - 4] = f0(j - 4)
        else:
            t_src[j - 7] = total
            t[j - 7] = t0(j - 7)
        send_apart(rt.at[1 - core, w], frt.at[w], fw_s, fw_r, at_col(sib))
        if j < 7:
            h, l = split2(rt[core, w, :])
            ih[par, w, :] = h
            il[par, w, :] = l
        if j == 1:
            D[1]()
        if j == 3:
            E[0]()
        if j == 4:
            D[3]()
            E[1]()
        if j == 5:
            D[4]()
            f[0] = f1(0, f[0])
        if j == 6:
            f[1] = f1(1, f[1])
            D[5]()
            E[3]()
            D[6]()
            for k in range(4):
                store_cover(128 * k, 256 * (k // 2), d_gy[k % 2, :, :, k // 2].reshape(128, 256))
    f[1] = f2(1, f[1])
    E[4]()
    t[0] = t1(0, t[0])
    h, l = split2(rt[core, 112:128, :])
    ih[par, 112:128, :] = h
    il[par, 112:128, :] = l
    f[0] = f3(0, f[0])
    f[2] = f2(2, f[2])
    t[1] = t1(1, t[1])
    f[1] = f3(1, f[1])
    E[5]()
    t[0] = t2(0, t[0])
    f[0] = f4(0, f[0])
    f[2] = f3(2, f[2])
    E[6]()
    for k in range(4):
        for r in range(4):
            for i in range(2):
                for n in range(2):
                    unit = e_gy[k % 2, r, 2 * i + n, k // 2]
                    xg[k, 16 * r + 8 * i : 16 * r + 8 * i + 8, 128 * n : 128 * n + 128] = unit
    t[1] = t2(1, t[1])
    f[1] = f4(1, f[1])
    f[2] = f4(2, f[2])
    arrived(starts)
    vectors = jnp.concatenate([rst[k] for k in range(4)], 1)
    forwards = Waits(frt, fw_s, fw_r)
    pending.append(forwards)
    forwards.wait_recv()
    split_rows(dia, frt)
    for j in range(3):
        arrived(f[j])
        for k in range(4):
            for i in range(2):
                for n in range(2):
                    r = 64 + 16 * j + 8 * i
                    xg[k, r : r + 8, 128 * n : 128 * n + 128] = f_gy[j, k % 2, 2 * i + n, k // 2]
    for j in range(2):
        arrived(t[j])
        for k in range(4):
            r = 112 + 8 * j
            xg[k, r : r + 8, :] = t_rx[j, k] + t_rx[j, 4 + k]
    across, below = xg[2:4].reshape(256, 256), xg[0:2].reshape(256, 256)
    upper, below = across + below.T, below + across.T
    store_cover(0, 256, upper[:128])
    store_cover(128, 256, upper[128:])
    store_cover(256, 0, below[:128])
    store_cover(384, 0, below[128:])

    def step(vectors):
        products = times_cover(vectors, g1, g2, g3)
        return orthonormal(outer_gram(products), products)

    vectors = lax.fori_loop(0, STEPS - 1, lambda i, v: step(v)[0], vectors)

    vh, vl = split2(vectors)
    vb = jnp.concatenate([vh, vl], 0)
    images = []
    for n in range(PIECES):
        o = pl.ds(IW * n, IW)
        h = jnp.concatenate([ih[k, :, o] for k in range(4)], 0)
        l = jnp.concatenate([il[k, :, o] for k in range(4)], 0)
        both = dot(vb, h)
        part = both[:16] + (both[16:] + dot(vh, l))
        img[n] = part
        limg[n, c] = part
        images.append(send_apart(img.at[n], limg.at[n, c], im_s.at[0], im_r.at[n], at_col(par)))
        send_apart(img.at[n], limg.at[n, c], im_s.at[1], im_r.at[PIECES], at_col(sib))
        if n == PIECES - 1:
            direct = send_apart(img.at[n], limg.at[n, c], im_s.at[2], im_r.at[PIECES + 1], at_col(dia))
    vectors, diagonal = step(vectors)
    for k in range(4):
        vs[k] = vectors[:, 128 * k : 128 * k + 128]
    right_o[...] = vs[c]
    eye = lax.broadcasted_iota(jnp.int32, (16, 128), 0) == lax.broadcasted_iota(jnp.int32, (16, 128), 1)
    str_o[...] = jnp.sum(jnp.where(eye, diagonal / rows_total, 0.0), 0, keepdims=True)[:, :16]

    for n in range(PIECES):
        images[n].wait_recv()
        if n < PIECES - 1:
            send_apart(limg.at[n, par], limg.at[n, par], if_s, if_r, at_col(sib))
    local, relays = Waits(img, im_s.at[1], im_r.at[PIECES]), Waits(img.at[: PIECES - 1], if_s, if_r)
    local.wait_recv()
    direct.wait_recv()
    relays.wait_recv()
    for n in range(PIECES):
        for k in range(4):
            left_o[:, 2048 * k + IW * n : 2048 * k + IW * n + IW] = limg[n, k]
    pending += [local, relays, direct, Waits(img, im_s.at[0], im_s.at[0])]
    pending.append(Waits(tab.at[0, :2], ex_s, ex_s))
    pending.append(Waits(tab.at[0, :4, pl.ds(0, 2 * sent[0])], all_s, all_s))
    for cp in pending:
        cp.wait_send()


def write_out(a, b, d, ao, bo, do, sem):
    copies = [pltpu.make_async_copy(x, o, sem.at[i]) for i, (x, o) in enumerate(((a, ao), (b, bo), (d, do)))]
    for cp in copies:
        cp.start()
    for cp in copies:
        cp.wait()


def scattered_scratch(*unit):
    V = pltpu.VMEM
    return [
        V((4, 4, *unit), f32),
        V((3, 4, *unit), f32),
        V((4, *unit), f32),
        V((3, *unit), f32),
        V(unit, f32),
        V((4, *unit), f32),
        V((4, 2, *unit), f32),
        V((2, 4, 4, 2, *unit), f32),
    ]


def on_device(rows_total, table, start):
    V, D = pltpu.VMEM, pltpu.SemaphoreType.DMA
    scratch = [
        V((2, 4, 2048, 128), f32),
        V((4, 128, 2048), f32),
        V((2, 128, 2048), f32),
        V((128, 2048), f32),
        V((128, 2048), f32),
        V((2, 2048, 256), bf16),
        V((2, 2048, 256), bf16),
        V((4, 128, 2048), bf16),
        V((4, 128, 2048), bf16),
        V((4, 16, 128), f32),
        *scattered_scratch(8, 256),
        *scattered_scratch(8, 128),
        V((3, 4, 8, 128), f32),
        V((3, 3, 8, 128), f32),
        V((3, 8, 128), f32),
        V((3, 4, 8, 128), f32),
        V((3, 8, 128), f32),
        V((3, 4, 8, 128), f32),
        V((3, 2, 8, 128), f32),
        V((3, 2, 4, 2, 8, 128), f32),
        V((2, 8, 256), f32),
        V((2, 4, 8, 256), f32),
        V((2, 8, 256), f32),
        V((2, 4, 8, 256), f32),
        V((2, 8, 256), f32),
        V((2, 8, 8, 256), f32),
        V((4, 128, 256), f32),
        V((512, 512), bf16),
        V((512, 512), bf16),
        V((512, 512), bf16),
        V((PIECES, 16, IW), f32),
        V((PIECES, 4, 16, IW), f32),
        V((4, 16, 128), f32),
        D((7,)),
        D, D,
        D, D((4,)),
        D, D,
        D, D((CHUNKS + 1, 2)),
        D, D,
        D,
        D((7,)), D((7,)), D((7,)),
        D((2,)), D((5,)), D((5,)),
        D((3,)), D((PIECES + 2,)),
        D, D,
    ]
    table, start = (pltpu.with_memory_space_constraint(x, pltpu.HBM) for x in (table, start))
    results = pl.pallas_call(
        functools.partial(kernel, rows_total),
        out_shape=[V((16, 128), f32), V((16, 8192), f32), V((1, 16), f32)],
        in_specs=[pl.BlockSpec(memory_space=pltpu.HBM)] * 2,
        out_specs=[pl.BlockSpec(memory_space=V)] * 3,
        scratch_shapes=scratch,
        compiler_params=pltpu.CompilerParams(
            collective_id=0, has_side_effects=True, vmem_limit_bytes=48 * 1024 * 1024
        ),
    )(table, start)
    right, left, strengths = pl.pallas_call(
        write_out,
        out_shape=[jax.ShapeDtypeStruct(x.shape, f32) for x in results],
        in_specs=[pl.BlockSpec(memory_space=V)] * 3,
        out_specs=[pl.BlockSpec(memory_space=pl.ANY)] * 3,
        scratch_shapes=[D((3,))],
        compiler_params=pltpu.CompilerParams(vmem_limit_bytes=1024 * 1024),
    )(*results)
    return right, left, strengths.reshape(16)


def solution(mesh):
    rows_total = 8192 * mesh.shape["rowa"] * mesh.shape["rowb"]
    return jax.shard_map(
        functools.partial(on_device, rows_total),
        mesh=mesh,
        in_specs=(P(("rowa", "rowb"), "col"), P(None, "col")),
        out_specs=(P(None, "col"), P(None, ("rowa", "rowb")), P()),
        check_vma=False,
    )
```

time: 84 us -> 80.4 us (0.957)
  Pallas kernels: 83.2 us -> 79.6 us
    pallas_call x1, Pallas kernels: 82.4 us -> 78.8 us  [on_device(): pl.pallas_call(functools.partial(kernel, rows_total), out_shape=[V((16, 1...]
where the time goes in v3:
time: 80.4 us; the launch traced here: 80.3 us
  Pallas kernels  79.6 us (99%)
    pallas_call x1, Pallas kernels, on_device(): pl.pallas_call(functools.partial(kernel, rows_total), out_shape=[V((16, 1...  78.8 us

profile of v3, /device:TPU:1, one launch (start us, length us, event | category | flops | bytes accessed | tf_op | source)
XLA Modules:
  0.0 80.3 jit_solution(5030041097915016353)
XLA Ops:
  0.6 78.8 %shard_map.49 = (f32[16,128]{1,0:T(8,128)S(1)}, f32[16,8192]{1,0:T(8,128)S(1)}, f32[1,16]{1,0:T(1,128)S(1)}) custom-call(f32[8192,128]{1,0:T(8,128)} %table.1, f32[16,128]{1,0:T(8,128)} %start.1), custom_call_target="tpu_custom_call" | custom-call | tf_op jit(solution)/shard_map/pallas_call | solution.py:588
  79.4 0.8 %shard_map.50 = (f32[16,128]{1,0:T(8,128)}, f32[16,8192]{1,0:T(8,128)}, f32[1,16]{1,0:T(1,128)}) custom-call(f32[16,128]{1,0:T(8,128)S(1)} %get-tuple-element.9.a, f32[16,8192]{1,0:T(8,128)S(1)} %get-tuple-element.10.b, f32[1,16]{1,0:T(1,128)S(1)} %get-tuple-element.11.d), custom_call_target="tpu_custom_call" | custom-call | tf_op jit(solution)/shard_map/pallas_call | solution.py:598

commit v4 on v3

--- a/solution.py
+++ b/solution.py
@@ -14,6 +14,7 @@
 bf16 = jnp.bfloat16
 WIDTHS = (16, 16, 16, 16, 16, 16, 16, 8, 8)
 CHUNKS = len(WIDTHS)
+LAST = (((0, 0, 2048),), ((1, 0, 1024), (2, 1024, 1024)))
 PIECES = 8
 IW = 2048 // PIECES
 
@@ -73,14 +74,16 @@
 def kernel(
     rows_total,
     table, start, right_o, left_o, str_o,
-    tab, tt, rt, stt, frt, wh, wl, ih, il, rst,
+    tab, tt, rt, stt, frt, r8, wh, wl, ih, il, rst,
     d_src, d_ry, d_sy, d_rz, d_sx, d_rx, d_gz, d_gy,
     e_src, e_ry, e_sy, e_rz, e_sx, e_rx, e_gz, e_gy,
     f_src, f_ry, f_sy, f_rz, f_sx, f_rx, f_gz, f_gy,
-    t_src, t_ry, t_sy, t_rz, t_sx, t_rx, xg,
+    t_src, t_ry, t_sy, t_rz, t_sx, t_rx,
+    u_src, u_ry, u_sy, u_rz, u_sx, u_rx,
+    c_src, c_ry, c_sy, c_rz, c_sx, c_rx, xg,
     g1, g2, g3, img, limg, vs,
     load_s, st_l, st_r, nat_s, nat_r, tq_s, tq_r, ex_s, ex_r, fw_s, fw_r,
-    all_s, y_r, z_r, x_r, az_r, ay_r, pair_r,
+    all_s, y_r, z_r, x_r, az_r, ay_r, pair_r, r8_r, c_s, c_r, r8f_s, r8f_r,
     im_s, im_r, if_s, if_r,
 ):
     ra, rb, c = lax.axis_index("rowa"), lax.axis_index("rowb"), lax.axis_index("col")
@@ -179,11 +182,10 @@
 
     def send_chunk(j, k):
         w = columns(j)
-        if (j, k) == (CHUNKS - 1, 1):
-            halves = [(ex_s, ex_r.at[j + i, k], pl.ds(1024 * i, 1024)) for i in range(2)]
-            exchange[j, k] = [
-                send_apart(tt.at[other + k, w, o], rt.at[k, w, o], s, r, at_col(par)) for s, r, o in halves
-            ]
+        if j == CHUNKS - 1:
+            for i, o, n in LAST[k]:
+                part = pl.ds(o, n)
+                send_apart(tt.at[other + k, w, part], r8.at[core, k, :, part], ex_s, r8_r.at[core, i], at_col(3 - 2 * half))
             return
         exchange[j, k] = [send_apart(tt.at[other + k, w], rt.at[k, w], ex_s, ex_r.at[j, k], at_col(par))]
 
@@ -315,23 +317,72 @@
         whole = f_gy.at[i, core]
         return sends([(whole, whole)], pair_r.at[2 + i], pair, whole)
 
+    T = (
+        (t_src, t_ry, t_sy, t_rz, t_sx, t_rx),
+        (u_src, u_ry, u_sy, u_rz, u_sx, u_rx),
+    )
+
     def t0(i):
-        t_ry[i, y] = t_src[i]
-        return sends([(t_src.at[i], t_ry.at[i, y])] * 3, y_r.at[5 + i], ys, t_ry.at[i, three])
+        src, ry = T[i][:2]
+        ry[y] = src[...]
+        return sends([(src, ry.at[y])] * 3, y_r.at[4 + i], ys, ry.at[three])
 
     def t1(i, cps):
+        ry, sy, rz = T[i][1:4]
         arrived(cps)
-        total = (t_ry[i, 0] + t_ry[i, 1]) + (t_ry[i, 2] + t_ry[i, 3])
-        t_sy[i] = total
-        t_rz[i, z] = total
-        return sends([(t_sy.at[i], t_rz.at[i, z])] * 3, z_r.at[5 + i], zs, t_rz.at[i, three])
+        total = (ry[0] + ry[1]) + (ry[2] + ry[3])
+        sy[...] = total
+        rz[z] = total
+        return sends([(sy, rz.at[z])] * 3, z_r.at[4 + i], zs, rz.at[three])
 
     def t2(i, cps):
+        rz, sx, rx = T[i][3:]
         arrived(cps)
-        total = (t_rz[i, 0] + t_rz[i, 1]) + (t_rz[i, 2] + t_rz[i, 3])
-        t_sx[i] = total
-        t_rx[i, spot] = total
-        return sends([(t_sx.at[i], t_rx.at[i, spot])] * 7, x_r.at[5 + i], xs, t_rx.at[i, seven])
+        total = (rz[0] + rz[1]) + (rz[2] + rz[3])
+        sx[...] = total
+        rx[spot] = total
+        return sends([(sx, rx.at[spot])] * 7, x_r.at[4 + i], xs, rx.at[seven])
+
+    def on_core_1(stage):
+        pl.when(core == 1)(stage)
+
+    def c_send(a, b, i, devs):
+        for dev in devs:
+            send_apart(a, b, c_s, c_r.at[i], dev)
+
+    def last_part(k, o, total):
+        x = r8[:, k, :, pl.ds(o, 1024)].reshape(16, 1024)
+        h = x.astype(bf16).astype(f32)
+        both = jnp.concatenate([h, x - h], 0).astype(bf16)
+        a, b = dot(both, wh[k, pl.ds(o, 1024), :]), dot(both, wl[k, pl.ds(o, 1024), :])
+        return total + (a[:16] + ((a[16:] + b[:16]) + b[16:]))
+
+    def c0():
+        total = jnp.zeros((16, 256), f32)
+        for k in range(2):
+            for i, o, n in LAST[k]:
+                for q in range(2):
+                    Waits(r8.at[q, k, :, pl.ds(o, n)], ex_s, r8_r.at[q, i]).wait_recv()
+                for first in range(o, o + n, 1024):
+                    total = last_part(k, first, total)
+        c_src[...] = total
+        c_ry[y] = total
+        c_send(c_src, c_ry.at[y], 0, ys)
+        send_apart(r8.at[:, 0], r8.at[:, 0], r8f_s, r8f_r, at_col(sib))
+
+    def c1():
+        Waits(c_ry.at[three], c_s, c_r.at[0]).wait_recv()
+        total = (c_ry[0] + c_ry[1]) + (c_ry[2] + c_ry[3])
+        c_sy[...] = total
+        c_rz[z] = total
+        c_send(c_sy, c_rz.at[z], 1, zs)
+
+    def c2():
+        Waits(c_rz.at[three], c_s, c_r.at[1]).wait_recv()
+        total = (c_rz[0] + c_rz[1]) + (c_rz[2] + c_rz[3])
+        c_sx[...] = total
+        c_rx[spot2] = total
+        c_send(c_sx, c_rx.at[spot2], 2, xs)
 
     D[0]()
     split_rows(c, tt.at[mine + core])
@@ -364,27 +415,22 @@
     for j in range(CHUNKS):
         w = columns(j)
         last = j == CHUNKS - 1
+        if last:
+            on_core_1(c0)
+            break
         arrived(exchange[j, 0])
         total = chunk_part(j, 0, 0, 2)
         if j == 5:
             E[2]()
-        if last:
-            arrived(exchange[j, 1][:1])
-            total = total + chunk_part(j, 1, 0, 1)
-            f[2] = f1(2, f[2])
-            arrived(exchange[j, 1][1:])
-            total = total + chunk_part(j, 1, 1024, 1)
-        else:
-            arrived(exchange[j, 1])
+        arrived(exchange[j, 1])
         if j == 2:
             D[2]()
         if j == 6:
             f[0] = f2(0, f[0])
         for k in range(2):
             issue(2 * j + 4 + k)
-        if not last:
-            total = total + chunk_part(j, 1, 0, 2)
-        if j < 7:
+        total = total + chunk_part(j, 1, 0, 2)
+        if j < 6:
             for i in range(2):
                 for n in range(2):
                     unit = total[8 * i : 8 * i + 8, 128 * n : 128 * n + 128]
@@ -395,8 +441,8 @@
             if j >= 4:
                 f[j - 4] = f0(j - 4)
         else:
-            t_src[j - 7] = total
-            t[j - 7] = t0(j - 7)
+            T[j - 6][0][...] = total
+            t[j - 6] = t0(j - 6)
         send_apart(rt.at[1 - core, w], frt.at[w], fw_s, fw_r, at_col(sib))
         if j < 7:
             h, l = split2(rt[core, w, :])
@@ -419,20 +465,30 @@
             D[6]()
             for k in range(4):
                 store_cover(128 * k, 256 * (k // 2), d_gy[k % 2, :, :, k // 2].reshape(128, 256))
+    t[0] = t1(0, t[0])
     f[1] = f2(1, f[1])
+    t[1] = t1(1, t[1])
+    on_core_1(c1)
+    t[0] = t2(0, t[0])
     E[4]()
-    t[0] = t1(0, t[0])
+    f[0] = f3(0, f[0])
+    f[1] = f3(1, f[1])
+    t[1] = t2(1, t[1])
+    on_core_1(c2)
+    E[5]()
+    f[0] = f4(0, f[0])
+    f[1] = f4(1, f[1])
+    forwards = Waits(frt.at[:120], fw_s, fw_r)
+    pending.append(forwards)
+    forwards.wait_recv()
+    to_core_0 = Waits(r8.at[:, 0], r8f_s, r8f_r)
+    pl.when(core == 0)(to_core_0.wait_recv)
+    frt[120:128, :] = r8[1 - core, core]
+    rt[core, 120:128, :] = r8[core, core]
+    split_rows(dia, frt)
     h, l = split2(rt[core, 112:128, :])
     ih[par, 112:128, :] = h
     il[par, 112:128, :] = l
-    f[0] = f3(0, f[0])
-    f[2] = f2(2, f[2])
-    t[1] = t1(1, t[1])
-    f[1] = f3(1, f[1])
-    E[5]()
-    t[0] = t2(0, t[0])
-    f[0] = f4(0, f[0])
-    f[2] = f3(2, f[2])
     E[6]()
     for k in range(4):
         for r in range(4):
@@ -440,16 +496,9 @@
                 for n in range(2):
                     unit = e_gy[k % 2, r, 2 * i + n, k // 2]
                     xg[k, 16 * r + 8 * i : 16 * r + 8 * i + 8, 128 * n : 128 * n + 128] = unit
-    t[1] = t2(1, t[1])
-    f[1] = f4(1, f[1])
-    f[2] = f4(2, f[2])
     arrived(starts)
     vectors = jnp.concatenate([rst[k] for k in range(4)], 1)
-    forwards = Waits(frt, fw_s, fw_r)
-    pending.append(forwards)
-    forwards.wait_recv()
-    split_rows(dia, frt)
-    for j in range(3):
+    for j in range(2):
         arrived(f[j])
         for k in range(4):
             for i in range(2):
@@ -458,9 +507,14 @@
                     xg[k, r : r + 8, 128 * n : 128 * n + 128] = f_gy[j, k % 2, 2 * i + n, k // 2]
     for j in range(2):
         arrived(t[j])
+        rx = T[j][5]
         for k in range(4):
-            r = 112 + 8 * j
-            xg[k, r : r + 8, :] = t_rx[j, k] + t_rx[j, 4 + k]
+            xg[k, columns(6 + j), :] = rx[k] + rx[4 + k]
+    on_core_1(Waits(c_rx.at[three], c_s, c_r.at[2]).wait_recv)
+    pl.when(core == 0)(Waits(c_rx, c_s, c_r.at[2]).wait_recv)
+    for k in range(4):
+        i = pl.ds(8 * (k % 2), 8)
+        xg[k, 120:128, :] = c_rx[k // 2, i] + c_rx[2 + k // 2, i]
     across, below = xg[2:4].reshape(256, 256), xg[0:2].reshape(256, 256)
     upper, below = across + below.T, below + across.T
     store_cover(0, 256, upper[:128])
@@ -509,6 +563,8 @@
             left_o[:, 2048 * k + IW * n : 2048 * k + IW * n + IW] = limg[n, k]
     pending += [local, relays, direct, Waits(img, im_s.at[0], im_s.at[0])]
     pending.append(Waits(tab.at[0, :2], ex_s, ex_s))
+    on_core_1(Waits(tab.at[0, :4, pl.ds(0, 2 * 52)], c_s, c_s).wait_send)
+    on_core_1(to_core_0.wait_send)
     pending.append(Waits(tab.at[0, :4, pl.ds(0, 2 * sent[0])], all_s, all_s))
     for cp in pending:
         cp.wait_send()
@@ -544,6 +600,7 @@
         V((2, 128, 2048), f32),
         V((128, 2048), f32),
         V((128, 2048), f32),
+        V((2, 2, 8, 2048), f32),
         V((2, 2048, 256), bf16),
         V((2, 2048, 256), bf16),
         V((4, 128, 2048), bf16),
@@ -551,20 +608,32 @@
         V((4, 16, 128), f32),
         *scattered_scratch(8, 256),
         *scattered_scratch(8, 128),
-        V((3, 4, 8, 128), f32),
-        V((3, 3, 8, 128), f32),
-        V((3, 8, 128), f32),
-        V((3, 4, 8, 128), f32),
-        V((3, 8, 128), f32),
-        V((3, 4, 8, 128), f32),
-        V((3, 2, 8, 128), f32),
-        V((3, 2, 4, 2, 8, 128), f32),
-        V((2, 8, 256), f32),
-        V((2, 4, 8, 256), f32),
-        V((2, 8, 256), f32),
-        V((2, 4, 8, 256), f32),
-        V((2, 8, 256), f32),
-        V((2, 8, 8, 256), f32),
+        V((2, 4, 8, 128), f32),
+        V((2, 3, 8, 128), f32),
+        V((2, 8, 128), f32),
+        V((2, 4, 8, 128), f32),
+        V((2, 8, 128), f32),
+        V((2, 4, 8, 128), f32),
+        V((2, 2, 8, 128), f32),
+        V((2, 2, 4, 2, 8, 128), f32),
+        V((16, 256), f32),
+        V((4, 16, 256), f32),
+        V((16, 256), f32),
+        V((4, 16, 256), f32),
+        V((16, 256), f32),
+        V((8, 16, 256), f32),
+        V((8, 256), f32),
+        V((4, 8, 256), f32),
+        V((8, 256), f32),
+        V((4, 8, 256), f32),
+        V((8, 256), f32),
+        V((8, 8, 256), f32),
+        V((16, 256), f32),
+        V((4, 16, 256), f32),
+        V((16, 256), f32),
+        V((4, 16, 256), f32),
+        V((16, 256), f32),
+        V((4, 16, 256), f32),
         V((4, 128, 256), f32),
         V((512, 512), bf16),
         V((512, 512), bf16),
@@ -576,11 +645,12 @@
         D, D,
         D, D((4,)),
         D, D,
-        D, D((CHUNKS + 1, 2)),
+        D, D((CHUNKS - 1, 2)),
         D, D,
         D,
-        D((7,)), D((7,)), D((7,)),
-        D((2,)), D((5,)), D((5,)),
+        D((6,)), D((6,)), D((6,)),
+        D((2,)), D((4,)), D((4,)),
+        D((2, 3)), D, D((3,)), D, D,
         D((3,)), D((PIECES + 2,)),
         D, D,
     ]

time: 80.4 us -> 79.1 us (0.984)
  Pallas kernels: 79.6 us -> 78.4 us
    pallas_call x1, Pallas kernels: 78.8 us -> 77.6 us  [on_device(): pl.pallas_call(functools.partial(kernel, rows_total), out_shape=[V((16, 1...]
where the time goes in v4:
time: 79.1 us; the launch traced here: 79 us
  Pallas kernels  78.4 us (99%)
    pallas_call x1, Pallas kernels, on_device(): pl.pallas_call(functools.partial(kernel, rows_total), out_shape=[V((16, 1...  77.6 us

profile of v4, /device:TPU:1, one launch (start us, length us, event | category | flops | bytes accessed | tf_op | source)
XLA Modules:
  0.0 79.0 jit_solution(11886420741694108717)
XLA Ops:
  0.6 77.6 %shard_map.49 = (f32[16,128]{1,0:T(8,128)S(1)}, f32[16,8192]{1,0:T(8,128)S(1)}, f32[1,16]{1,0:T(1,128)S(1)}) custom-call(f32[8192,128]{1,0:T(8,128)} %table.1, f32[16,128]{1,0:T(8,128)} %start.1), custom_call_target="tpu_custom_call" | custom-call | tf_op jit(solution)/shard_map/pallas_call | solution.py:658
  78.2 0.8 %shard_map.50 = (f32[16,128]{1,0:T(8,128)}, f32[16,8192]{1,0:T(8,128)}, f32[1,16]{1,0:T(1,128)}) custom-call(f32[16,128]{1,0:T(8,128)S(1)} %get-tuple-element.9.a, f32[16,8192]{1,0:T(8,128)S(1)} %get-tuple-element.10.b, f32[1,16]{1,0:T(1,128)S(1)} %get-tuple-element.11.d), custom_call_target="tpu_custom_call" | custom-call | tf_op jit(solution)/shard_map/pallas_call | solution.py:668

commit v5 on v4

--- a/solution.py
+++ b/solution.py
@@ -78,7 +78,7 @@
     d_src, d_ry, d_sy, d_rz, d_sx, d_rx, d_gz, d_gy,
     e_src, e_ry, e_sy, e_rz, e_sx, e_rx, e_gz, e_gy,
     f_src, f_ry, f_sy, f_rz, f_sx, f_rx, f_gz, f_gy,
-    t_src, t_ry, t_sy, t_rz, t_sx, t_rx,
+    t_src, t_ry, t_sy, t_rz, t_sx, t_rx, t_gy,
     u_src, u_ry, u_sy, u_rz, u_sx, u_rx,
     c_src, c_ry, c_sy, c_rz, c_sx, c_rx, xg,
     g1, g2, g3, img, limg, vs,
@@ -342,6 +342,19 @@
         sx[...] = total
         rx[spot] = total
         return sends([(sx, rx.at[spot])] * 7, x_r.at[4 + i], xs, rx.at[seven])
+
+    def t2_equal(cps):
+        arrived(cps)
+        total = (t_rz[0] + t_rz[1]) + (t_rz[2] + t_rz[3])
+        t_sx[...] = total
+        t_rx[spot2] = total
+        return sends([(t_sx, t_rx.at[spot2])] * 3, x_r.at[4], xs2, t_rx.at[three])
+
+    def t3_equal(cps):
+        arrived(cps)
+        t_gy[core] = t_rx[:2] + t_rx[2:]
+        whole = t_gy.at[core]
+        return sends([(whole, whole)], pair_r.at[4], pair, whole)
 
     def on_core_1(stage):
         pl.when(core == 1)(stage)
@@ -462,22 +475,23 @@
             f[1] = f1(1, f[1])
             D[5]()
             E[3]()
-            D[6]()
-            for k in range(4):
-                store_cover(128 * k, 256 * (k // 2), d_gy[k % 2, :, :, k // 2].reshape(128, 256))
     t[0] = t1(0, t[0])
     f[1] = f2(1, f[1])
     t[1] = t1(1, t[1])
     on_core_1(c1)
-    t[0] = t2(0, t[0])
+    t[0] = t2_equal(t[0])
     E[4]()
     f[0] = f3(0, f[0])
     f[1] = f3(1, f[1])
     t[1] = t2(1, t[1])
     on_core_1(c2)
+    D[6]()
+    for k in range(4):
+        store_cover(128 * k, 256 * (k // 2), d_gy[k % 2, :, :, k // 2].reshape(128, 256))
     E[5]()
     f[0] = f4(0, f[0])
     f[1] = f4(1, f[1])
+    t[0] = t3_equal(t[0])
     forwards = Waits(frt.at[:120], fw_s, fw_r)
     pending.append(forwards)
     forwards.wait_recv()
@@ -505,11 +519,12 @@
                 for n in range(2):
                     r = 64 + 16 * j + 8 * i
                     xg[k, r : r + 8, 128 * n : 128 * n + 128] = f_gy[j, k % 2, 2 * i + n, k // 2]
-    for j in range(2):
-        arrived(t[j])
-        rx = T[j][5]
-        for k in range(4):
-            xg[k, columns(6 + j), :] = rx[k] + rx[4 + k]
+    arrived(t[0])
+    for k in range(4):
+        xg[k, columns(6), :] = t_gy[k % 2, k // 2]
+    arrived(t[1])
+    for k in range(4):
+        xg[k, columns(7), :] = u_rx[k] + u_rx[4 + k]
     on_core_1(Waits(c_rx.at[three], c_s, c_r.at[2]).wait_recv)
     pl.when(core == 0)(Waits(c_rx, c_s, c_r.at[2]).wait_recv)
     for k in range(4):
@@ -621,7 +636,8 @@
         V((16, 256), f32),
         V((4, 16, 256), f32),
         V((16, 256), f32),
-        V((8, 16, 256), f32),
+        V((4, 16, 256), f32),
+        V((2, 2, 16, 256), f32),
         V((8, 256), f32),
         V((4, 8, 256), f32),
         V((8, 256), f32),
@@ -649,7 +665,7 @@
         D, D,
         D,
         D((6,)), D((6,)), D((6,)),
-        D((2,)), D((4,)), D((4,)),
+        D((2,)), D((4,)), D((5,)),
         D((2, 3)), D, D((3,)), D, D,
         D((3,)), D((PIECES + 2,)),
         D, D,

time: 79.1 us -> 79.1 us (level)
  no operation moved by 1% of the time
where the time goes in v5:
time: 79.1 us; the launch traced here: 79 us
  Pallas kernels  78.4 us (99%)
    pallas_call x1, Pallas kernels, on_device(): pl.pallas_call(functools.partial(kernel, rows_total), out_shape=[V((16, 1...  77.6 us

profile of v5, /device:TPU:1, one launch (start us, length us, event | category | flops | bytes accessed | tf_op | source)
XLA Modules:
  0.0 79.0 jit_solution(14316307566477446607)
XLA Ops:
  0.6 77.6 %shard_map.49 = (f32[16,128]{1,0:T(8,128)S(1)}, f32[16,8192]{1,0:T(8,128)S(1)}, f32[1,16]{1,0:T(1,128)S(1)}) custom-call(f32[8192,128]{1,0:T(8,128)} %table.1, f32[16,128]{1,0:T(8,128)} %start.1), custom_call_target="tpu_custom_call" | custom-call | tf_op jit(solution)/shard_map/pallas_call | solution.py:674
  78.2 0.8 %shard_map.50 = (f32[16,128]{1,0:T(8,128)}, f32[16,8192]{1,0:T(8,128)}, f32[1,16]{1,0:T(1,128)}) custom-call(f32[16,128]{1,0:T(8,128)S(1)} %get-tuple-element.9.a, f32[16,8192]{1,0:T(8,128)S(1)} %get-tuple-element.10.b, f32[1,16]{1,0:T(1,128)S(1)} %get-tuple-element.11.d), custom_call_target="tpu_custom_call" | custom-call | tf_op jit(solution)/shard_map/pallas_call | solution.py:684

commit v6 on v4

--- a/solution.py
+++ b/solution.py
@@ -82,7 +82,7 @@
     u_src, u_ry, u_sy, u_rz, u_sx, u_rx,
     c_src, c_ry, c_sy, c_rz, c_sx, c_rx, xg,
     g1, g2, g3, img, limg, vs,
-    load_s, st_l, st_r, nat_s, nat_r, tq_s, tq_r, ex_s, ex_r, fw_s, fw_r,
+    far, load_s, st_l, st_r, nat_s, nat_r, tq_s, tq_r, ex_s, ex_r, fw_s, fw_r,
     all_s, y_r, z_r, x_r, az_r, ay_r, pair_r, r8_r, c_s, c_r, r8f_s, r8f_r,
     im_s, im_r, if_s, if_r,
 ):
@@ -160,12 +160,13 @@
     loads += [load(4 + i, q, 0, 2048) for i, q in enumerate((other + 1, mine, mine + 1))]
     own_start.start()
 
+    def signal(sem, dev):
+        pl.semaphore_signal(sem, inc=1, device_id=dev, device_id_type=MESH)
+
     barrier = pltpu.get_barrier_semaphore()
-    for d in (1, 2, 3):
-        pl.semaphore_signal(barrier, inc=1, device_id=at_y(d), device_id_type=MESH)
-        pl.semaphore_signal(barrier, inc=1, device_id=at_z(d), device_id_type=MESH)
-    for da, dc in XP:
-        pl.semaphore_signal(barrier, inc=1, device_id=at_x(da, dc), device_id_type=MESH)
+    near = [at_x(0, 1), at_x(0, 2), at_x(0, 3), at_x(1, 2), at_x(1, 3), at_y(1), at_y(3), at_z(1), at_z(3)]
+    for dev in near:
+        signal(barrier, dev)
 
     def transpose_rows(q, first, blocks):
         def body(i, carry):
@@ -193,7 +194,9 @@
         loads[p].wait()
         transpose_rows(other, 512 * p, 2)
         if p == 0:
-            pl.semaphore_wait(barrier, 13)
+            pl.semaphore_wait(barrier, len(near))
+            for dev in (at_x(0, 2), at_y(1), at_z(1)):
+                signal(far, dev)
         o = pl.ds(512 * p, 512)
         send_apart(tt.at[other, columns(0), o], rt.at[0, columns(0), o], ex_s, ex_r.at[0, 0], at_col(par))
     whole = rt.at[0, columns(0)]
@@ -384,6 +387,7 @@
         c_rx[spot2] = total
         c_send(c_sx, c_rx.at[spot2], 2, xs)
 
+    pl.semaphore_wait(far, 3)
     D[0]()
     split_rows(c, tt.at[mine + core])
     tq.wait_recv()
@@ -462,9 +466,6 @@
             f[1] = f1(1, f[1])
             D[5]()
             E[3]()
-            D[6]()
-            for k in range(4):
-                store_cover(128 * k, 256 * (k // 2), d_gy[k % 2, :, :, k // 2].reshape(128, 256))
     t[0] = t1(0, t[0])
     f[1] = f2(1, f[1])
     t[1] = t1(1, t[1])
@@ -475,6 +476,9 @@
     f[1] = f3(1, f[1])
     t[1] = t2(1, t[1])
     on_core_1(c2)
+    D[6]()
+    for k in range(4):
+        store_cover(128 * k, 256 * (k // 2), d_gy[k % 2, :, :, k // 2].reshape(128, 256))
     E[5]()
     f[0] = f4(0, f[0])
     f[1] = f4(1, f[1])
@@ -641,6 +645,7 @@
         V((PIECES, 16, IW), f32),
         V((PIECES, 4, 16, IW), f32),
         V((4, 16, 128), f32),
+        pltpu.SemaphoreType.REGULAR,
         D((7,)),
         D, D,
         D, D((4,)),

time: 79.1 us -> 78.8 us (level)
  no operation moved by 1% of the time
where the time goes in v6:
time: 78.8 us; the launch traced here: 78.7 us
  Pallas kernels  78.1 us (99%)
    pallas_call x1, Pallas kernels, on_device(): pl.pallas_call(functools.partial(kernel, rows_total), out_shape=[V((16, 1...  77.2 us

profile of v6, /device:TPU:1, one launch (start us, length us, event | category | flops | bytes accessed | tf_op | source)
XLA Modules:
  0.0 78.7 jit_solution(10162494337324893459)
XLA Ops:
  0.6 77.2 %shard_map.49 = (f32[16,128]{1,0:T(8,128)S(1)}, f32[16,8192]{1,0:T(8,128)S(1)}, f32[1,16]{1,0:T(1,128)S(1)}) custom-call(f32[8192,128]{1,0:T(8,128)} %table.1, f32[16,128]{1,0:T(8,128)} %start.1), custom_call_target="tpu_custom_call" | custom-call | tf_op jit(solution)/shard_map/pallas_call | solution.py:663
  77.9 0.8 %shard_map.50 = (f32[16,128]{1,0:T(8,128)}, f32[16,8192]{1,0:T(8,128)}, f32[1,16]{1,0:T(1,128)}) custom-call(f32[16,128]{1,0:T(8,128)S(1)} %get-tuple-element.9.a, f32[16,8192]{1,0:T(8,128)S(1)} %get-tuple-element.10.b, f32[1,16]{1,0:T(1,128)S(1)} %get-tuple-element.11.d), custom_call_target="tpu_custom_call" | custom-call | tf_op jit(solution)/shard_map/pallas_call | solution.py:673

commit v7 on v6

--- a/solution.py
+++ b/solution.py
@@ -554,17 +554,22 @@
     eye = lax.broadcasted_iota(jnp.int32, (16, 128), 0) == lax.broadcasted_iota(jnp.int32, (16, 128), 1)
     str_o[...] = jnp.sum(jnp.where(eye, diagonal / rows_total, 0.0), 0, keepdims=True)[:, :16]
 
+    def put(n, k):
+        left_o[:, pl.ds(pl.multiple_of(2048 * k + IW * n, IW), IW)] = limg[n, k]
+
     for n in range(PIECES):
         images[n].wait_recv()
         if n < PIECES - 1:
             send_apart(limg.at[n, par], limg.at[n, par], if_s, if_r, at_col(sib))
+        put(n, c)
+        put(n, par)
     local, relays = Waits(img, im_s.at[1], im_r.at[PIECES]), Waits(img.at[: PIECES - 1], if_s, if_r)
     local.wait_recv()
     direct.wait_recv()
     relays.wait_recv()
     for n in range(PIECES):
-        for k in range(4):
-            left_o[:, 2048 * k + IW * n : 2048 * k + IW * n + IW] = limg[n, k]
+        put(n, sib)
+        put(n, dia)
     pending += [local, relays, direct, Waits(img, im_s.at[0], im_s.at[0])]
     pending.append(Waits(tab.at[0, :2], ex_s, ex_s))
     on_core_1(Waits(tab.at[0, :4, pl.ds(0, 2 * 52)], c_s, c_s).wait_send)

time: 78.8 us -> 78.8 us (level)
  no operation moved by 1% of the time
where the time goes in v7:
time: 78.8 us; the launch traced here: 78.7 us
  Pallas kernels  78.1 us (99%)
    pallas_call x1, Pallas kernels, on_device(): pl.pallas_call(functools.partial(kernel, rows_total), out_shape=[V((16, 1...  77.2 us

profile of v7, /device:TPU:1, one launch (start us, length us, event | category | flops | bytes accessed | tf_op | source)
XLA Modules:
  0.0 78.7 jit_solution(14759194895441737257)
XLA Ops:
  0.6 77.2 %shard_map.49 = (f32[16,128]{1,0:T(8,128)S(1)}, f32[16,8192]{1,0:T(8,128)S(1)}, f32[1,16]{1,0:T(1,128)S(1)}) custom-call(f32[8192,128]{1,0:T(8,128)} %table.1, f32[16,128]{1,0:T(8,128)} %start.1), custom_call_target="tpu_custom_call" | custom-call | tf_op jit(solution)/shard_map/pallas_call | solution.py:668
  77.9 0.8 %shard_map.50 = (f32[16,128]{1,0:T(8,128)}, f32[16,8192]{1,0:T(8,128)}, f32[1,16]{1,0:T(1,128)}) custom-call(f32[16,128]{1,0:T(8,128)S(1)} %get-tuple-element.9.a, f32[16,8192]{1,0:T(8,128)S(1)} %get-tuple-element.10.b, f32[1,16]{1,0:T(1,128)S(1)} %get-tuple-element.11.d), custom_call_target="tpu_custom_call" | custom-call | tf_op jit(solution)/shard_map/pallas_call | solution.py:678
